TPU v7x, 256 devices: a whole 4x4x8 slice. The times are simulated.
256 devices in a mesh: obs: 32 (over y, z), chan: 8 (over x, core).
Axes of the slice: x: 4, y: 4, z: 8, core: 2. Of those that a mesh axis runs over, the one named last changes fastest.
Arguments:
- jacobian: bfloat16 [8192, 256, 137], P('obs', 'chan'), may hold values from -0.5 to 0.5
- departures: float32 [256, 8192], P('chan', 'obs'), may hold values from -6 to 6
- obs_weights: float32 [256, 8192], P('chan', 'obs'), may hold values from 0.25 to 4
- column_count: int32 [32], P('obs'), may hold values from 1 to 256, as said below
- grid_block: int32 [64], P('obs'), may hold values from 0 to 63, as said below
- sqrt_cov: float32 [137, 137], replicated, may hold values from -0.5 to 0.5
Outputs:
- increment: float32 [8192, 137], P('obs')
- residual: float32 [8192, 137], P('obs')
Inputs may be any that keep to these rules, and one draw needn't show every extreme that they name: The first column_count of a device's 256 column slots are observed; some device has all 256 observed in every draw. `grid_block`: the owner of grid block g is index g // 2 of obs. The 2 blocks of one device match blocks of 2 different owners; in every draw some owner has a block matched by each device (every device matches one of that owner's blocks), and some device matches that owner's last block.
All inputs are finite; a program needn't handle non-finite values.
Results may differ from a plain program's by a relative error of at most 0.02.
Values may be sent and summed in bfloat16 or wider, within the bound.
A program may use at most 64 MiB of HBM per device.

v0:
```python
import functools

import jax
import jax.numpy as jnp
from jax import lax
from jax.sharding import Mesh
from jax.sharding import PartitionSpec as P

BLOCK = 128
ITERS = 5
GRID_BLK = 2
OBS = ("obs_0", "obs_1")
CHAN = ("chan_0", "chan_1")
OBS_CHAN = ("obs_0", "obs_1", "chan_0", "chan_1")


def from_everyone(value, axis):
    copies = jnp.broadcast_to(value, (lax.axis_size(axis), *value.shape))
    return lax.all_to_all(copies, axis, split_axis=0, concat_axis=0, tiled=True)


def joined_along(tiles, dim):
    tiles = jnp.moveaxis(tiles, 0, dim)
    lengths = tiles.shape
    return tiles.reshape(*lengths[:dim], lengths[dim] * lengths[dim + 1], *lengths[dim + 2 :])


def collect(value, axis, dim):
    tiles = from_everyone(value, axis)
    return joined_along(tiles, dim)


def cut_along(value, dim, peers):
    before, after = (value.shape[:dim], value.shape[dim + 1 :])
    return jnp.moveaxis(value.reshape(*before, peers, -1, *after), dim, 0)


def sum_at_owner(value, axis, dim):
    tiles = cut_along(value, dim, lax.axis_size(axis))
    arrived = lax.all_to_all(tiles, axis, split_axis=0, concat_axis=0, tiled=True)
    return arrived.sum(axis=0)


def one_axis_at_a_time(value, axes):
    return functools.reduce(lax.psum, axes, value)


def side_by_side(arrays, axis, dim, along):
    widths = [a.shape[along] for a in arrays]
    both = jnp.concatenate(arrays, axis=along)
    whole = lax.all_gather(both, axis, axis=dim, tiled=True)
    return tuple(jnp.split(whole, [sum(widths[:k]) for k in range(1, len(widths))], axis=along))


def block_terms(jac_part, weight_part, mask_part, predicted):
    scaled = (mask_part[:, None] * weight_part * predicted).astype(jnp.bfloat16)
    return lax.dot_general(
        jac_part, scaled, (((1,), (1,)), ((0,), (0,))), preferred_element_type=jnp.float32
    )


def forward_terms(jac_part, weight_part, mask_part, field_part):
    predicted = lax.dot_general(
        jac_part, field_part, (((2,), (1,)), ((0,), (0,))), preferred_element_type=jnp.float32
    )
    return block_terms(jac_part, weight_part, mask_part, predicted)


def per_device(jacobian, departures, obs_weights, column_count, grid_block, sqrt_cov):
    obs_count = lax.axis_size(OBS)
    chan_count = lax.axis_size(CHAN)
    myself = lax.axis_index(OBS)
    capacity, group_channels, layers = jacobian.shape
    block_count = capacity // BLOCK
    weight_cols = obs_weights.T
    depart_cols = departures.T
    observed = (jnp.arange(capacity, dtype=jnp.int32) < column_count[0]).astype(jnp.float32)
    every_id = collect(grid_block, OBS, 0).reshape(obs_count, block_count)
    targets = jnp.arange(obs_count, dtype=jnp.int32)
    send_pick = (grid_block[None, :] // GRID_BLK == targets[:, None]).astype(jnp.float32)
    owned_here = every_id // GRID_BLK == myself
    places = every_id % GRID_BLK
    grid_index = jnp.arange(GRID_BLK, dtype=jnp.int32)
    take_pick = jnp.sum(
        ((places[None] == grid_index[:, None, None]) & owned_here[None]).astype(jnp.float32), axis=2
    )
    share_cols = BLOCK // chan_count

    def local_terms(kernel_fn, inputs):
        return kernel_fn(jacobian, weight_cols, observed, inputs)

    def to_owners(terms):
        blocked = terms.reshape(block_count, BLOCK, layers)
        blocked = sum_at_owner(blocked, CHAN, 1)
        outgoing = jnp.dot(send_pick, blocked.reshape(block_count, -1))
        incoming = lax.all_to_all(
            outgoing.reshape(obs_count, share_cols, layers),
            OBS,
            split_axis=0,
            concat_axis=0,
            tiled=True,
        )
        summed = jnp.dot(take_pick, incoming.reshape(obs_count, -1))
        return summed.reshape(GRID_BLK, share_cols, layers)

    def spread(field):
        return jnp.dot(field.reshape(-1, layers), sqrt_cov).reshape(field.shape)

    def spread_back(field):
        flat = lax.dot_general(field.reshape(-1, layers), sqrt_cov, (((1,), (1,)), ((), ())))
        return flat.reshape(field.shape)

    def squared(values):
        partial_sum = jnp.sum(values * values)
        return one_axis_at_a_time(partial_sum, OBS_CHAN)

    residual = spread_back(to_owners(local_terms(block_terms, depart_cols)))
    control = jnp.zeros_like(residual)
    direction = residual
    norm_now = squared(residual)
    for iteration in range(ITERS):
        rounded = spread(direction).astype(jnp.bfloat16).reshape(GRID_BLK, -1)
        to_outgoing = jnp.dot(
            take_pick.T.astype(jnp.bfloat16), rounded, preferred_element_type=jnp.float32
        ).astype(jnp.bfloat16)
        to_incoming = lax.all_to_all(
            to_outgoing.reshape(obs_count, share_cols, layers),
            OBS,
            split_axis=0,
            concat_axis=0,
            tiled=True,
        )
        picked = jnp.dot(
            send_pick.T.astype(jnp.bfloat16),
            to_incoming.reshape(obs_count, -1),
            preferred_element_type=jnp.float32,
        )
        picked = picked.astype(jnp.bfloat16).reshape(block_count, share_cols, layers)
        picked = collect(picked, CHAN, 1)
        fetched = picked.reshape(capacity, layers)
        image = direction + spread_back(to_owners(local_terms(forward_terms, fetched)))
        curvature_partial_sum = jnp.sum(direction * image)
        step_length = norm_now / one_axis_at_a_time(curvature_partial_sum, OBS_CHAN)
        control = control + step_length * direction
        residual = residual - step_length * image
        norm_next = squared(residual)
        direction = residual + norm_next / norm_now * direction
        norm_now = norm_next
    increment = spread(control)
    increment, residual = tuple(
        (
            part.astype(jnp.float32)
            for part in side_by_side(
                (increment.astype(jnp.bfloat16), residual.astype(jnp.bfloat16)), CHAN, 1, 0
            )
        )
    )
    return (increment.reshape(-1, layers), residual.reshape(-1, layers))


def solution(mesh):
    split = Mesh(mesh.devices.reshape(4, 8, 4, 2), ("obs_0", "obs_1", "chan_0", "chan_1"))
    return jax.shard_map(
        per_device,
        mesh=split,
        in_specs=(P(OBS, CHAN, None), P(CHAN, OBS), P(CHAN, OBS), P(OBS), P(OBS), P()),
        out_specs=(P(OBS, None), P(OBS, None)),
        check_vma=False,
    )
```

profile of v0, /device:TPU:1, one launch (start us, length us, event | category | flops | bytes accessed | tf_op | source)
XLA Modules:
  0.0 729.1 jit_solution(8434426794626697605)
XLA Ops:
  2.0 12.0 %all-to-all-start = ((s32[32,1,2]{2,1,0:T(1,128)}), s32[32,1,2]{2,1,0:T(1,128)S(1)}, u32[]{:S(2)}, u32[]{:S(2)}) async-start(s32[32,1,2]{2,1,0:T(1,128)} %broadcast_in_dim.12), calls=%async_computation | async-start | bytes 32768 | tf_op jit(solution)/shard_map/all_to_all | solution.py:19
  16.1 2.5 fusion.5
  19.5 3.1 all-to-all-done
  22.6 6.4 all-to-all-start.1
  29.1 6.4 all-to-all-done.1
  36.9 5.4 all-to-all-start.2
  42.4 9.6 %all-to-all-done.2 = bf16[32,16,137]{2,1,0:T(8,128)(2,1)S(1)} async-done(((bf16[32,16,137]{2,1,0:T(8,128)(2,1)}), bf16[32,16,137]{2,1,0:T(8,128)(2,1)S(1)}, u32[]{:S(2)}, u32[]{:S(2)}) %all-to-all-start.2) | async-done | bytes 140320 | tf_op jit(solution)/shard_map/all_to_all | solution.py:96
  54.6 15.6 %all_to_all.119 = bf16[32,16,137]{2,1,0:T(8,128)(2,1)S(1)} all-to-all(bf16[32,16,137]{2,1,0:T(8,128)(2,1)S(1)} %reshape.249), channel_id=1, replica_groups=mesh['obs_0'=4,'obs_1'=8,'chan_0'=4,'chan_1'=2] {'obs_0','obs_1'}, dimensions={0} | all-to-all | bytes 280576 | tf_op jit(solution)/shard_map/all_to_all | solution.py:126
  70.9 11.3 %all_to_all.120 = bf16[8,2,16,137]{3,2,1,0:T(8,128)(2,1)S(1)} all-to-all(bf16[8,2,16,137]{3,2,1,0:T(8,128)(2,1)S(1)} %broadcast_in_dim.13), channel_id=1, replica_groups=mesh['obs_0'=4,'obs_1'=8,'chan_0'=4,'chan_1'=2] {'chan_0','chan_1'}, dimensions={0} | all-to-all | bytes 140288 | tf_op jit(solution)/shard_map/all_to_all | solution.py:19
  84.1 9.7 %all_to_all.121 = f32[8,2,16,137]{3,2,1,0:T(8,128)S(1)} all-to-all(f32[8,2,16,137]{3,2,1,0:T(8,128)S(1)} %copy.98), channel_id=1, replica_groups=mesh['obs_0'=4,'obs_1'=8,'chan_0'=4,'chan_1'=2] {'chan_0','chan_1'}, dimensions={0} | all-to-all | bytes 280576 | tf_op jit(solution)/shard_map/all_to_all | solution.py:40
  94.6 13.7 %all_to_all.122 = bf16[32,16,137]{2,1,0:T(8,128)(2,1)S(1)} all-to-all(bf16[32,16,137]{2,1,0:T(8,128)(2,1)S(1)} %copy.100), channel_id=1, replica_groups=mesh['obs_0'=4,'obs_1'=8,'chan_0'=4,'chan_1'=2] {'obs_0','obs_1'}, dimensions={0} | all-to-all | bytes 280576 | tf_op jit(solution)/shard_map/all_to_all | solution.py:96
  110.3 8.4 %all-reduce.2 = (f32[]{:T(128)}, f32[]{:T(128)}) all-reduce(f32[]{:T(128)} %get-tuple-element.26, f32[]{:T(128)} %get-tuple-element.28), channel_id=1, replica_groups=mesh['obs_0'=4,'obs_1'=8,'chan_0'=4,'chan_1'=2] {'obs_0'}, use_global_device_ids=true, to_apply=%region_3.4 | all-reduce | flops 2 | bytes 16 | tf_op jit(solution)/shard_map/psum | solution.py:45
  118.7 12.9 %all-reduce = (f32[]{:T(128)}, f32[]{:T(128)}) all-reduce(f32[]{:T(128)} %get-tuple-element.16, f32[]{:T(128)} %get-tuple-element.17), channel_id=1, replica_groups=mesh['obs_0'=4,'obs_1'=8,'chan_0'=4,'chan_1'=2] {'obs_1'}, use_global_device_ids=true, to_apply=%region_4.5 | all-reduce | flops 2 | bytes 16 | tf_op jit(solution)/shard_map/psum | solution.py:45
  131.6 7.5 %all-reduce.1 = (f32[]{:T(128)}, f32[]{:T(128)}) all-reduce(f32[]{:T(128)} %get-tuple-element.12, f32[]{:T(128)} %get-tuple-element.13), channel_id=1, replica_groups=mesh['obs_0'=4,'obs_1'=8,'chan_0'=4,'chan_1'=2] {'chan_0'}, use_global_device_ids=true, to_apply=%region_5.6 | all-reduce | flops 2 | bytes 16 | tf_op jit(solution)/shard_map/psum | solution.py:45
  139.1 13.1 %all-reduce.3 = (f32[]{:T(128)}, f32[]{:T(128)}) all-reduce(f32[]{:T(128)} %get-tuple-element.14, f32[]{:T(128)} %get-tuple-element.15), channel_id=1, replica_groups=mesh['obs_0'=4,'obs_1'=8,'chan_0'=4,'chan_1'=2] {'chan_1'}, use_global_device_ids=true, to_apply=%region_6.7 | all-reduce | flops 2 | bytes 16 | tf_op jit(solution)/shard_map/psum | solution.py:45
  154.2 7.2 psum.288
  161.3 11.3 %psum.289 = f32[]{:T(128)} all-reduce(f32[]{:T(128)} %psum.288), channel_id=1, replica_groups=mesh['obs_0'=4,'obs_1'=8,'chan_0'=4,'chan_1'=2] {'obs_1'}, use_global_device_ids=true, to_apply=%region_15.16 | all-reduce | flops 1 | bytes 8 | tf_op jit(solution)/shard_map/psum | solution.py:45
  172.7 7.3 psum.290
  179.9 10.8 %psum.291 = f32[]{:T(128)} all-reduce(f32[]{:T(128)} %psum.290), channel_id=1, replica_groups=mesh['obs_0'=4,'obs_1'=8,'chan_0'=4,'chan_1'=2] {'chan_1'}, use_global_device_ids=true, to_apply=%region_17.18 | all-reduce | flops 1 | bytes 8 | tf_op jit(solution)/shard_map/psum | solution.py:45
  193.3 14.7 %all_to_all.123 = bf16[32,16,137]{2,1,0:T(8,128)(2,1)S(1)} all-to-all(bf16[32,16,137]{2,1,0:T(8,128)(2,1)S(1)} %reshape.255), channel_id=1, replica_groups=mesh['obs_0'=4,'obs_1'=8,'chan_0'=4,'chan_1'=2] {'obs_0','obs_1'}, dimensions={0} | all-to-all | bytes 280576 | tf_op jit(solution)/shard_map/all_to_all | solution.py:126
  208.7 11.6 %all_to_all.124 = bf16[8,2,16,137]{3,2,1,0:T(8,128)(2,1)S(1)} all-to-all(bf16[8,2,16,137]{3,2,1,0:T(8,128)(2,1)S(1)} %broadcast_in_dim.14), channel_id=1, replica_groups=mesh['obs_0'=4,'obs_1'=8,'chan_0'=4,'chan_1'=2] {'chan_0','chan_1'}, dimensions={0} | all-to-all | bytes 140288 | tf_op jit(solution)/shard_map/all_to_all | solution.py:19
  222.2 9.7 %all_to_all.125 = f32[8,2,16,137]{3,2,1,0:T(8,128)S(1)} all-to-all(f32[8,2,16,137]{3,2,1,0:T(8,128)S(1)} %copy.104), channel_id=1, replica_groups=mesh['obs_0'=4,'obs_1'=8,'chan_0'=4,'chan_1'=2] {'chan_0','chan_1'}, dimensions={0} | all-to-all | bytes 280576 | tf_op jit(solution)/shard_map/all_to_all | solution.py:40
  232.7 13.6 %all_to_all.126 = bf16[32,16,137]{2,1,0:T(8,128)(2,1)S(1)} all-to-all(bf16[32,16,137]{2,1,0:T(8,128)(2,1)S(1)} %copy.106), channel_id=1, replica_groups=mesh['obs_0'=4,'obs_1'=8,'chan_0'=4,'chan_1'=2] {'obs_0','obs_1'}, dimensions={0} | all-to-all | bytes 280576 | tf_op jit(solution)/shard_map/all_to_all | solution.py:96
  248.4 8.4 %psum.292 = f32[]{:T(128)} all-reduce(f32[]{:T(128)} %get-tuple-element.30), channel_id=1, replica_groups=mesh['obs_0'=4,'obs_1'=8,'chan_0'=4,'chan_1'=2] {'obs_0'}, use_global_device_ids=true, to_apply=%region_20.21 | all-reduce | flops 1 | bytes 8 | tf_op jit(solution)/shard_map/psum | solution.py:45
  256.8 12.9 %psum.293 = f32[]{:T(128)} all-reduce(f32[]{:T(128)} %psum.292), channel_id=1, replica_groups=mesh['obs_0'=4,'obs_1'=8,'chan_0'=4,'chan_1'=2] {'obs_1'}, use_global_device_ids=true, to_apply=%region_21.22 | all-reduce | flops 1 | bytes 8 | tf_op jit(solution)/shard_map/psum | solution.py:45
  269.6 7.5 %psum.294 = f32[]{:T(128)} all-reduce(f32[]{:T(128)} %psum.293), channel_id=1, replica_groups=mesh['obs_0'=4,'obs_1'=8,'chan_0'=4,'chan_1'=2] {'chan_0'}, use_global_device_ids=true, to_apply=%region_22.23 | all-reduce | flops 1 | bytes 8 | tf_op jit(solution)/shard_map/psum | solution.py:45
  277.1 13.1 %psum.295 = f32[]{:T(128)} all-reduce(f32[]{:T(128)} %psum.294), channel_id=1, replica_groups=mesh['obs_0'=4,'obs_1'=8,'chan_0'=4,'chan_1'=2] {'chan_1'}, use_global_device_ids=true, to_apply=%region_23.24 | all-reduce | flops 1 | bytes 8 | tf_op jit(solution)/shard_map/psum | solution.py:45
  292.2 7.2 psum.296
  299.4 11.3 %psum.297 = f32[]{:T(128)} all-reduce(f32[]{:T(128)} %psum.296), channel_id=1, replica_groups=mesh['obs_0'=4,'obs_1'=8,'chan_0'=4,'chan_1'=2] {'obs_1'}, use_global_device_ids=true, to_apply=%region_26.27 | all-reduce | flops 1 | bytes 8 | tf_op jit(solution)/shard_map/psum | solution.py:45
  310.7 7.3 psum.298
  318.0 10.8 %psum.299 = f32[]{:T(128)} all-reduce(f32[]{:T(128)} %psum.298), channel_id=1, replica_groups=mesh['obs_0'=4,'obs_1'=8,'chan_0'=4,'chan_1'=2] {'chan_1'}, use_global_device_ids=true, to_apply=%region_28.29 | all-reduce | flops 1 | bytes 8 | tf_op jit(solution)/shard_map/psum | solution.py:45
  331.4 14.7 %all_to_all.127 = bf16[32,16,137]{2,1,0:T(8,128)(2,1)S(1)} all-to-all(bf16[32,16,137]{2,1,0:T(8,128)(2,1)S(1)} %reshape.261), channel_id=1, replica_groups=mesh['obs_0'=4,'obs_1'=8,'chan_0'=4,'chan_1'=2] {'obs_0','obs_1'}, dimensions={0} | all-to-all | bytes 280576 | tf_op jit(solution)/shard_map/all_to_all | solution.py:126
  346.8 11.3 %all_to_all.128 = bf16[8,2,16,137]{3,2,1,0:T(8,128)(2,1)S(1)} all-to-all(bf16[8,2,16,137]{3,2,1,0:T(8,128)(2,1)S(1)} %broadcast_in_dim.15), channel_id=1, replica_groups=mesh['obs_0'=4,'obs_1'=8,'chan_0'=4,'chan_1'=2] {'chan_0','chan_1'}, dimensions={0} | all-to-all | bytes 140288 | tf_op jit(solution)/shard_map/all_to_all | solution.py:19
  360.0 9.7 %all_to_all.129 = f32[8,2,16,137]{3,2,1,0:T(8,128)S(1)} all-to-all(f32[8,2,16,137]{3,2,1,0:T(8,128)S(1)} %copy.110), channel_id=1, replica_groups=mesh['obs_0'=4,'obs_1'=8,'chan_0'=4,'chan_1'=2] {'chan_0','chan_1'}, dimensions={0} | all-to-all | bytes 280576 | tf_op jit(solution)/shard_map/all_to_all | solution.py:40
  370.5 13.6 %all_to_all.130 = bf16[32,16,137]{2,1,0:T(8,128)(2,1)S(1)} all-to-all(bf16[32,16,137]{2,1,0:T(8,128)(2,1)S(1)} %copy.112), channel_id=1, replica_groups=mesh['obs_0'=4,'obs_1'=8,'chan_0'=4,'chan_1'=2] {'obs_0','obs_1'}, dimensions={0} | all-to-all | bytes 280576 | tf_op jit(solution)/shard_map/all_to_all | solution.py:96
  386.2 8.4 %psum.300 = f32[]{:T(128)} all-reduce(f32[]{:T(128)} %get-tuple-element.32), channel_id=1, replica_groups=mesh['obs_0'=4,'obs_1'=8,'chan_0'=4,'chan_1'=2] {'obs_0'}, use_global_device_ids=true, to_apply=%region_31.32 | all-reduce | flops 1 | bytes 8 | tf_op jit(solution)/shard_map/psum | solution.py:45
  394.6 12.9 %psum.301 = f32[]{:T(128)} all-reduce(f32[]{:T(128)} %psum.300), channel_id=1, replica_groups=mesh['obs_0'=4,'obs_1'=8,'chan_0'=4,'chan_1'=2] {'obs_1'}, use_global_device_ids=true, to_apply=%region_32.33 | all-reduce | flops 1 | bytes 8 | tf_op jit(solution)/shard_map/psum | solution.py:45
  407.4 7.5 %psum.302 = f32[]{:T(128)} all-reduce(f32[]{:T(128)} %psum.301), channel_id=1, replica_groups=mesh['obs_0'=4,'obs_1'=8,'chan_0'=4,'chan_1'=2] {'chan_0'}, use_global_device_ids=true, to_apply=%region_33.34 | all-reduce | flops 1 | bytes 8 | tf_op jit(solution)/shard_map/psum | solution.py:45
  414.9 13.1 %psum.303 = f32[]{:T(128)} all-reduce(f32[]{:T(128)} %psum.302), channel_id=1, replica_groups=mesh['obs_0'=4,'obs_1'=8,'chan_0'=4,'chan_1'=2] {'chan_1'}, use_global_device_ids=true, to_apply=%region_34.35 | all-reduce | flops 1 | bytes 8 | tf_op jit(solution)/shard_map/psum | solution.py:45
  430.0 7.2 psum.304
  437.2 11.3 %psum.305 = f32[]{:T(128)} all-reduce(f32[]{:T(128)} %psum.304), channel_id=1, replica_groups=mesh['obs_0'=4,'obs_1'=8,'chan_0'=4,'chan_1'=2] {'obs_1'}, use_global_device_ids=true, to_apply=%region_37.38 | all-reduce | flops 1 | bytes 8 | tf_op jit(solution)/shard_map/psum | solution.py:45
  448.5 7.3 psum.306
  455.8 10.8 %psum.307 = f32[]{:T(128)} all-reduce(f32[]{:T(128)} %psum.306), channel_id=1, replica_groups=mesh['obs_0'=4,'obs_1'=8,'chan_0'=4,'chan_1'=2] {'chan_1'}, use_global_device_ids=true, to_apply=%region_39.40 | all-reduce | flops 1 | bytes 8 | tf_op jit(solution)/shard_map/psum | solution.py:45
  469.1 23.8 %all_to_all.131 = bf16[32,16,137]{2,1,0:T(8,128)(2,1)S(1)} all-to-all(bf16[32,16,137]{2,1,0:T(8,128)(2,1)S(1)} %reshape.267), channel_id=1, replica_groups=mesh['obs_0'=4,'obs_1'=8,'chan_0'=4,'chan_1'=2] {'obs_0','obs_1'}, dimensions={0} | all-to-all | bytes 280576 | tf_op jit(solution)/shard_map/all_to_all | solution.py:126
  493.7 11.3 %all_to_all.132 = bf16[8,2,16,137]{3,2,1,0:T(8,128)(2,1)S(1)} all-to-all(bf16[8,2,16,137]{3,2,1,0:T(8,128)(2,1)S(1)} %broadcast_in_dim.16), channel_id=1, replica_groups=mesh['obs_0'=4,'obs_1'=8,'chan_0'=4,'chan_1'=2] {'chan_0','chan_1'}, dimensions={0} | all-to-all | bytes 140288 | tf_op jit(solution)/shard_map/all_to_all | solution.py:19
  506.9 9.7 %all_to_all.133 = f32[8,2,16,137]{3,2,1,0:T(8,128)S(1)} all-to-all(f32[8,2,16,137]{3,2,1,0:T(8,128)S(1)} %copy.116), channel_id=1, replica_groups=mesh['obs_0'=4,'obs_1'=8,'chan_0'=4,'chan_1'=2] {'chan_0','chan_1'}, dimensions={0} | all-to-all | bytes 280576 | tf_op jit(solution)/shard_map/all_to_all | solution.py:40
  517.4 13.6 %all_to_all.134 = bf16[32,16,137]{2,1,0:T(8,128)(2,1)S(1)} all-to-all(bf16[32,16,137]{2,1,0:T(8,128)(2,1)S(1)} %copy.118), channel_id=1, replica_groups=mesh['obs_0'=4,'obs_1'=8,'chan_0'=4,'chan_1'=2] {'obs_0','obs_1'}, dimensions={0} | all-to-all | bytes 280576 | tf_op jit(solution)/shard_map/all_to_all | solution.py:96
  533.1 8.4 %psum.308 = f32[]{:T(128)} all-reduce(f32[]{:T(128)} %get-tuple-element.34), channel_id=1, replica_groups=mesh['obs_0'=4,'obs_1'=8,'chan_0'=4,'chan_1'=2] {'obs_0'}, use_global_device_ids=true, to_apply=%region_42.43 | all-reduce | flops 1 | bytes 8 | tf_op jit(solution)/shard_map/psum | solution.py:45
  541.5 12.9 %psum.309 = f32[]{:T(128)} all-reduce(f32[]{:T(128)} %psum.308), channel_id=1, replica_groups=mesh['obs_0'=4,'obs_1'=8,'chan_0'=4,'chan_1'=2] {'obs_1'}, use_global_device_ids=true, to_apply=%region_43.44 | all-reduce | flops 1 | bytes 8 | tf_op jit(solution)/shard_map/psum | solution.py:45
  554.3 7.5 %psum.310 = f32[]{:T(128)} all-reduce(f32[]{:T(128)} %psum.309), channel_id=1, replica_groups=mesh['obs_0'=4,'obs_1'=8,'chan_0'=4,'chan_1'=2] {'chan_0'}, use_global_device_ids=true, to_apply=%region_44.45 | all-reduce | flops 1 | bytes 8 | tf_op jit(solution)/shard_map/psum | solution.py:45
  561.8 13.1 %psum.311 = f32[]{:T(128)} all-reduce(f32[]{:T(128)} %psum.310), channel_id=1, replica_groups=mesh['obs_0'=4,'obs_1'=8,'chan_0'=4,'chan_1'=2] {'chan_1'}, use_global_device_ids=true, to_apply=%region_45.46 | all-reduce | flops 1 | bytes 8 | tf_op jit(solution)/shard_map/psum | solution.py:45
  576.9 7.2 psum.312
  584.1 11.3 %psum.313 = f32[]{:T(128)} all-reduce(f32[]{:T(128)} %psum.312), channel_id=1, replica_groups=mesh['obs_0'=4,'obs_1'=8,'chan_0'=4,'chan_1'=2] {'obs_1'}, use_global_device_ids=true, to_apply=%region_48.49 | all-reduce | flops 1 | bytes 8 | tf_op jit(solution)/shard_map/psum | solution.py:45
  595.4 7.3 psum.314
  602.7 10.8 %psum.315 = f32[]{:T(128)} all-reduce(f32[]{:T(128)} %psum.314), channel_id=1, replica_groups=mesh['obs_0'=4,'obs_1'=8,'chan_0'=4,'chan_1'=2] {'chan_1'}, use_global_device_ids=true, to_apply=%region_50.51 | all-reduce | flops 1 | bytes 8 | tf_op jit(solution)/shard_map/psum | solution.py:45
  616.0 14.7 %all_to_all.135 = bf16[32,16,137]{2,1,0:T(8,128)(2,1)S(1)} all-to-all(bf16[32,16,137]{2,1,0:T(8,128)(2,1)S(1)} %reshape.273), channel_id=1, replica_groups=mesh['obs_0'=4,'obs_1'=8,'chan_0'=4,'chan_1'=2] {'obs_0','obs_1'}, dimensions={0} | all-to-all | bytes 280576 | tf_op jit(solution)/shard_map/all_to_all | solution.py:126
  631.5 11.3 %all_to_all.136 = bf16[8,2,16,137]{3,2,1,0:T(8,128)(2,1)S(1)} all-to-all(bf16[8,2,16,137]{3,2,1,0:T(8,128)(2,1)S(1)} %broadcast_in_dim.34), channel_id=1, replica_groups=mesh['obs_0'=4,'obs_1'=8,'chan_0'=4,'chan_1'=2] {'chan_0','chan_1'}, dimensions={0} | all-to-all | bytes 140288 | tf_op jit(solution)/shard_map/all_to_all | solution.py:19
  644.7 9.7 %all_to_all.137 = f32[8,2,16,137]{3,2,1,0:T(8,128)S(1)} all-to-all(f32[8,2,16,137]{3,2,1,0:T(8,128)S(1)} %copy.122), channel_id=1, replica_groups=mesh['obs_0'=4,'obs_1'=8,'chan_0'=4,'chan_1'=2] {'chan_0','chan_1'}, dimensions={0} | all-to-all | bytes 280576 | tf_op jit(solution)/shard_map/all_to_all | solution.py:40
  655.2 13.6 %all_to_all.138 = bf16[32,16,137]{2,1,0:T(8,128)(2,1)S(1)} all-to-all(bf16[32,16,137]{2,1,0:T(8,128)(2,1)S(1)} %copy.124), channel_id=1, replica_groups=mesh['obs_0'=4,'obs_1'=8,'chan_0'=4,'chan_1'=2] {'obs_0','obs_1'}, dimensions={0} | all-to-all | bytes 280576 | tf_op jit(solution)/shard_map/all_to_all | solution.py:96
  670.9 8.4 %psum.316 = f32[]{:T(128)} all-reduce(f32[]{:T(128)} %get-tuple-element.36), channel_id=1, replica_groups=mesh['obs_0'=4,'obs_1'=8,'chan_0'=4,'chan_1'=2] {'obs_0'}, use_global_device_ids=true, to_apply=%region_53.54 | all-reduce | flops 1 | bytes 8 | tf_op jit(solution)/shard_map/psum | solution.py:45
  679.3 12.9 %psum.317 = f32[]{:T(128)} all-reduce(f32[]{:T(128)} %psum.316), channel_id=1, replica_groups=mesh['obs_0'=4,'obs_1'=8,'chan_0'=4,'chan_1'=2] {'obs_1'}, use_global_device_ids=true, to_apply=%region_54.55 | all-reduce | flops 1 | bytes 8 | tf_op jit(solution)/shard_map/psum | solution.py:45
  692.1 7.5 %psum.318 = f32[]{:T(128)} all-reduce(f32[]{:T(128)} %psum.317), channel_id=1, replica_groups=mesh['obs_0'=4,'obs_1'=8,'chan_0'=4,'chan_1'=2] {'chan_0'}, use_global_device_ids=true, to_apply=%region_55.56 | all-reduce | flops 1 | bytes 8 | tf_op jit(solution)/shard_map/psum | solution.py:45
  699.6 13.1 %psum.319 = f32[]{:T(128)} all-reduce(f32[]{:T(128)} %psum.318), channel_id=1, replica_groups=mesh['obs_0'=4,'obs_1'=8,'chan_0'=4,'chan_1'=2] {'chan_1'}, use_global_device_ids=true, to_apply=%region_56.57 | all-reduce | flops 1 | bytes 8 | tf_op jit(solution)/shard_map/psum | solution.py:45
  714.2 13.0 %all_gather.3 = bf16[4,128,137]{2,1,0:T(8,128)(2,1)S(1)} all-gather(bf16[4,16,137]{2,1,0:T(8,128)(2,1)S(1)} %pad_maximum_fusion), channel_id=1, replica_groups=mesh['obs_0'=4,'obs_1'=8,'chan_0'=4,'chan_1'=2] {'chan_0','chan_1'}, dimensions={1}, use_global_device_ids=true | all-gather | bytes 157824 | tf_op jit(solution)/shard_map/all_gather | solution.py:51
  (166 shorter events, 43.5 us)
Async XLA Ops:
  0.6 52.0 %copy-start = (f32[137,137]{1,0:T(8,128)S(1)}, f32[137,137]{1,0:T(8,128)}, u32[]{:S(2)}) copy-start(f32[137,137]{1,0:T(8,128)} %param.11) | copy-start | bytes 225232
  2.0 20.6 %all-to-all-start = ((s32[32,1,2]{2,1,0:T(1,128)}), s32[32,1,2]{2,1,0:T(1,128)S(1)}, u32[]{:S(2)}, u32[]{:S(2)}) async-start(s32[32,1,2]{2,1,0:T(1,128)} %broadcast_in_dim.12), calls=%async_computation | async-start | bytes 32768 | tf_op jit(solution)/shard_map/all_to_all | solution.py:19
  22.6 12.9 %all-to-all-start.1 = ((f32[8,2,16,137]{3,2,1,0:T(8,128)}), f32[8,2,16,137]{3,2,1,0:T(8,128)S(1)}, u32[]{:S(2)}, u32[]{:S(2)}) async-start(f32[8,2,16,137]{3,2,1,0:T(8,128)} %copy.94), calls=%async_computation.1 | async-start | bytes 524288 | tf_op jit(solution)/shard_map/all_to_all | solution.py:40
  36.9 45.4 %copy-start.1 = (bf16[256,32,137]{0,1,2:T(8,128)(2,1)S(1)}, bf16[256,32,137]{0,1,2:T(8,128)(2,1)}, u32[]{:S(2)}) copy-start(bf16[256,32,137]{0,1,2:T(8,128)(2,1)} %param.6) | copy-start | bytes 6733828
  36.9 15.1 %all-to-all-start.2 = ((bf16[32,16,137]{2,1,0:T(8,128)(2,1)}), bf16[32,16,137]{2,1,0:T(8,128)(2,1)S(1)}, u32[]{:S(2)}, u32[]{:S(2)}) async-start(bf16[32,16,137]{2,1,0:T(8,128)(2,1)} %copy.96), calls=%async_computation.2 | async-start | bytes 524288 | tf_op jit(solution)/shard_map/all_to_all | solution.py:96
  70.2 12.8 %copy-start.2 = (f32[32,256]{1,0:T(8,128)S(1)}, f32[32,256]{1,0:T(8,128)}, u32[]{:S(2)}) copy-start(f32[32,256]{1,0:T(8,128)} %param.8) | copy-start | bytes 98308
where the time goes:
time: 735 us; the launch traced here: 729 us
  blocking collectives  626 us (85%)
  starting transfers between devices  23.8 us (3%)
  local copies, waits for them, and re-layouts  20.6 us (3%)
  waiting for transfers between devices  19.1 us (3%)
  other arithmetic  14.7 us (2%)
  between operations  14.3 us (2%)
  matrix products  10.7 us (1%)
    psum x36, blocking collectives, one_axis_at_a_time(): return functools.reduce(lax.psum, axes, value)  356 us
    all_to_all x5, blocking collectives, per_device(): lax.all_to_all(to_outgoing.reshape(obs_count, share_cols, layers), OBS, s...  83.6 us
    all_to_all x5, blocking collectives, to_owners(): lax.all_to_all(outgoing.reshape(obs_count, share_cols, layers), OBS, spli...  68.1 us
    all_to_all x5, blocking collectives, from_everyone(): return lax.all_to_all(copies, axis, split_axis=0, concat_axis=0, tiled=True)  56.8 us
    all_to_all x5, blocking collectives, sum_at_owner(): lax.all_to_all(tiles, axis, split_axis=0, concat_axis=0, tiled=True)  48.7 us
  transfers between devices with their start and end apart: 3, of which 3 were waited for; matrix products, arithmetic and copies ran while one was open for 1% of the time, Pallas kernels for 0%

commit v1 on v0

v1 whole, which is shorter than its diff:
```python
import jax
import jax.numpy as jnp
from jax import lax
from jax.experimental import pallas as pl
from jax.experimental.pallas import tpu as pltpu
from jax.sharding import Mesh
from jax.sharding import PartitionSpec as P

ITERS = 5
L = 137
NY, NZ, NX, NC = 4, 8, 4, 2
NCH = NX * NC
NM = NY * NCH
LH = 35
CHUNKS = 5
PER = LH // CHUNKS
WIDE = LH * 128
ID_LANE = 200
OBS = ("obs_0", "obs_1")
CHAN = ("chan_0", "chan_1")
MESH = pl.DeviceIdType.MESH
F32 = jnp.float32
BF16 = jnp.bfloat16


def iota(shape, dim):
    return lax.broadcasted_iota(jnp.int32, shape, dim)


def dot(a, b):
    return jnp.dot(a, b, preferred_element_type=F32)


def dot_t(a, b):
    return lax.dot_general(a, b, (((1,), (1,)), ((), ())), preferred_element_type=F32)


def halves(v):
    hi = v.astype(BF16)
    return hi, (v - hi.astype(F32)).astype(BF16)


def lanes(q):
    return pl.ds(q * 128, 128)


def kernel(
    cnt_ref, gb_ref, jt_ref, w_ref, d_ref, s_ref,
    inc_ref, res_ref,
    sb, jr, mw, sd, fx, sv, ts, sh, sl, perm, eye, own, pick, ids,
    r, p, s, x, mz, sx, sz, out, got,
    js, jq, zs, zq, xs, xq, vs, vq, ys, yq, os, oq,
):
    my_y = lax.axis_index("obs_0")
    my_z = lax.axis_index("obs_1")
    my_x = lax.axis_index("chan_0")
    my_c = lax.axis_index("chan_1")
    my_m = my_y * NCH + my_x * NC + my_c

    def plane_peer(m):
        return (m // NCH, my_z, (m % NCH) // NC, m % NC)

    def ring_peer(z):
        return (my_y, z, my_x, my_c)

    barrier = pltpu.get_barrier_semaphore()

    def greet_plane(t, carry):
        pl.semaphore_signal(barrier, inc=1, device_id=plane_peer((my_m + t) % NM), device_id_type=MESH)
        return carry

    def greet_ring(t, carry):
        pl.semaphore_signal(barrier, inc=1, device_id=ring_peer((my_z + t) % NZ), device_id_type=MESH)
        return carry

    lax.fori_loop(1, NM, greet_plane, 0)
    lax.fori_loop(1, NZ, greet_ring, 0)

    row = iota((256, 256), 0)
    col = iota((256, 256), 1)
    perm[...] = jnp.where((row % 8) // 4 * 128 + (row // 8) * 4 + row % 4 == col, 1.0, 0.0).astype(BF16)
    eye[...] = jnp.where(row == col, 1.0, 0.0).astype(BF16)
    sh[...] = jnp.zeros_like(sh)
    sl[...] = jnp.zeros_like(sl)
    root_hi, root_lo = halves(s_ref[...])
    sh[0:L, 0:L] = root_hi
    sl[0:L, 0:L] = root_lo
    r4 = iota((8, 128), 0)
    ids[my_y] = jnp.where(r4 < 4, gb_ref[0], gb_ref[1]).astype(F32)
    mask = jnp.where(iota((32, 256), 1) < cnt_ref[0], 1.0, 0.0)
    weight = mask * w_ref[...]
    weight_hi, weight_lo = halves(weight)
    scaled_d = (weight * d_ref[...]).astype(BF16)

    pl.semaphore_wait(barrier, NM - 1 + NZ - 1)

    def id_copy(t):
        peer = (my_y + t) % NY
        return pltpu.make_async_remote_copy(
            src_ref=ids.at[my_y], dst_ref=ids.at[my_y], send_sem=ys.at[t], recv_sem=yq.at[my_y],
            device_id=(peer, my_z, my_x, my_c), device_id_type=MESH)

    def id_arrival(t):
        peer = (my_y + t) % NY
        return pltpu.make_async_remote_copy(
            src_ref=ids.at[peer], dst_ref=ids.at[peer], send_sem=ys.at[t], recv_sem=yq.at[peer],
            device_id=(peer, my_z, my_x, my_c), device_id_type=MESH)

    for t in range(1, NY):
        id_copy(t).start()

    for q in range(CHUNKS):
        def turn(i, carry):
            h = q * PER + i
            block = jt_ref[pl.ds(4 * h, 4)].reshape(128, 256)
            turned = dot_t(perm[...], block).astype(BF16)
            sb[:, :, pl.ds(pl.multiple_of(h * 128, 128), 128)] = turned.reshape(NM, 8, 128)
            return carry

        if q < CHUNKS - 1:
            lax.fori_loop(0, PER, turn, 0)
        else:
            lax.fori_loop(0, PER - 1, turn, 0)
            block = jnp.concatenate([jt_ref[L - 1], weight_hi, weight_lo, scaled_d], axis=0)
            turned = dot_t(perm[...], block).astype(BF16)
            sb[:, :, lanes(LH - 1)] = turned.reshape(NM, 8, 128)

        def send(t, carry):
            m = (my_m + t) % NM
            part = pl.ds(q * PER * 128, PER * 128)
            pltpu.make_async_remote_copy(
                src_ref=sb.at[m, :, part], dst_ref=jr.at[my_m, :, part],
                send_sem=js.at[m], recv_sem=jq.at[my_m],
                device_id=plane_peer(m), device_id_type=MESH).start()
            return carry

        lax.fori_loop(1, NM, send, 0)

    jr[my_m] = sb[my_m]

    for t in range(1, NY):
        id_arrival(t).wait()

    def j_arrival(m):
        return pltpu.make_async_remote_copy(
            src_ref=sb.at[m], dst_ref=jr.at[m], send_sem=js.at[m], recv_sem=jq.at[m],
            device_id=plane_peer(m), device_id_type=MESH)

    def arrive(t, carry):
        j_arrival((my_m + t) % NM).wait()
        return carry

    lax.fori_loop(1, NM, arrive, 0)

    lane = iota((8, 128), 1)
    lane2 = iota((8, 256), 1)
    row2 = iota((8, 256), 0)

    def across(v):
        v = v + pltpu.roll(v, 64, 1)
        return v + pltpu.roll(v, 32, 1)

    def unpack(m, carry):
        extra = jr[m, :, lanes(LH - 1)].astype(F32)
        mw[m] = across(jnp.where((lane >= 32) & (lane < 96), extra, 0.0))
        sd[m] = across(jnp.where(lane >= 96, extra, 0.0))
        return carry

    lax.fori_loop(0, NM, unpack, 0)

    for y in range(NY):
        ident = ids[y][:, 0:1]
        own[pl.ds(8 * y, 8), :] = jnp.where(
            (ident.astype(jnp.int32) == lane2 // 4) & (row2 % 4 == lane2 % 4), 1.0, 0.0)

    def ring_copy(buf, send_sem, recv_sem, slot, t):
        return pltpu.make_async_remote_copy(
            src_ref=buf.at[slot, my_z], dst_ref=buf.at[slot, my_z],
            send_sem=send_sem.at[slot, t], recv_sem=recv_sem.at[slot, my_z],
            device_id=ring_peer((my_z + t) % NZ), device_id_type=MESH)

    def ring_arrival(buf, send_sem, recv_sem, slot, t):
        z = (my_z + t) % NZ
        return pltpu.make_async_remote_copy(
            src_ref=buf.at[slot, z], dst_ref=buf.at[slot, z],
            send_sem=send_sem.at[slot, t], recv_sem=recv_sem.at[slot, z],
            device_id=ring_peer(z), device_id_type=MESH)

    FAR_FIRST = (4, 3, 5, 2, 6, 1, 7)

    def terms(factor, slot):
        def group(y, carry):
            acc = []
            for h in range(LH):
                total = None
                for c in range(NCH):
                    m = y * NCH + c
                    prod = jr[m, :, lanes(h)].astype(F32) * factor[m]
                    total = prod if total is None else total + prod
                acc.append(total)
            stacked = jnp.concatenate(acc, axis=0)
            hi, lo = halves(stacked)
            spot = jnp.where(iota((128, 128), 0) // 32 == iota((128, 128), 1) % 4, 1.0, 0.0).astype(BF16)
            sums = dot(hi, spot) + dot(lo, spot)
            first = jnp.zeros((8, 128), F32)
            second = jnp.zeros((8, 128), F32)
            for h in range(LH):
                piece = jnp.where(lane // 4 == h % 32, sums[8 * h: 8 * h + 8], 0.0)
                if h < 32:
                    first = first + piece
                else:
                    second = second + piece
            ts[y, :, 0:128] = first
            ts[y, :, 128:256] = second
            return carry

        lax.fori_loop(0, NY, group, 0)
        hi, lo = halves(ts[...].reshape(32, 256))
        back = dot_t(hi, sh[...]) + dot_t(lo, sh[...]) + dot_t(hi, sl[...])
        back = back.reshape(NY, 8, 256)
        back = jnp.where(iota((NY, 8, 256), 2) == ID_LANE, jnp.concatenate([ids[...]] * 2, axis=2), back)
        mz[slot, my_z] = back.reshape(32, 256).astype(BF16)
        for t in FAR_FIRST:
            ring_copy(mz, zs, zq, slot, t).start()

    def ring_wait(buf, send_sem, recv_sem, slot):
        for t in range(1, NZ):
            ring_arrival(buf, send_sem, recv_sem, slot, t).wait()

    terms(sd, 0)
    ring_wait(mz, zs, zq, 0)
    every = mz[0].reshape(256, 256)
    ident = every[:, ID_LANE: ID_LANE + 1].astype(F32).astype(jnp.int32)
    match = jnp.where((ident == col // 4) & (row % 4 == col % 4), 1.0, 0.0).astype(BF16)
    pick[...] = dot_t(eye[...], match).astype(BF16)
    body = jnp.where(col < L, dot(pick[...], every), 0.0)
    r[...] = body
    p[...] = jnp.zeros_like(body)
    s[...] = jnp.zeros_like(body)
    x[...] = jnp.zeros_like(body)

    def plane_copy(slot, t):
        m = (my_m + t) % NM
        return pltpu.make_async_remote_copy(
            src_ref=sx.at[slot, my_m], dst_ref=sx.at[slot, my_m],
            send_sem=xs.at[slot, m], recv_sem=xq.at[slot, my_m],
            device_id=plane_peer(m), device_id_type=MESH)

    def plane_arrival(slot, t):
        m = (my_m + t) % NM
        return pltpu.make_async_remote_copy(
            src_ref=sx.at[slot, m], dst_ref=sx.at[slot, m],
            send_sem=xs.at[slot, m], recv_sem=xq.at[slot, m],
            device_id=plane_peer(m), device_id_type=MESH)

    def iteration(i, carry):
        norm_old, step_old = carry
        slot = (i + 1) % 2
        res = r[...]
        hi, lo = halves(res)
        choose = own[...].astype(BF16)
        near_hi = dot(choose, hi).astype(BF16)
        near_lo = dot(choose, lo).astype(BF16)
        field = dot(near_hi, sh[...]) + dot(near_lo, sh[...]) + dot(near_hi, sl[...])
        field = field.astype(BF16).astype(F32).reshape(NY, 8, 256)
        ts[...] = field
        squares = jnp.sum(res * res, axis=0, keepdims=True)
        squares = squares[:, 0:128] + squares[:, 128:256]

        def predict(y, carry):
            for h in range(LH):
                base = ts[y, :, 0:128] if h < 32 else ts[y, :, 128:256]
                fx[:, lanes(h)] = jnp.take_along_axis(base, 4 * (h % 32) + lane // 32, axis=1)
            for c in range(NCH):
                m = y * NCH + c
                total = jnp.zeros((8, 128), F32)
                for h in range(LH):
                    total = total + jr[m, :, lanes(h)].astype(F32) * fx[:, lanes(h)]
                total = across(total)
                scaled = mw[m] * total
                sv[m] = scaled
                carry = carry + scaled * total
            return carry

        bends = lax.fori_loop(0, NY, predict, jnp.zeros((8, 128), F32))
        bends = jnp.sum(bends, axis=0, keepdims=True) * 0.25
        lane1 = iota((1, 128), 1)
        sx[slot, my_m] = jnp.where(
            lane1 < 64, squares + pltpu.roll(squares, 64, 1), bends + pltpu.roll(bends, 64, 1))

        def start(t, carry):
            plane_copy(slot, t).start()
            return carry

        lax.fori_loop(1, NM, start, 0)
        terms(sv, slot)

        def finish(t, carry):
            plane_arrival(slot, t).wait()
            return carry

        lax.fori_loop(1, NM, finish, 0)
        plane = jnp.sum(sx[slot], axis=0)
        sz[slot, my_z] = plane
        for t in FAR_FIRST:
            ring_copy(sz, vs, vq, slot, t).start()
        ring_wait(mz, zs, zq, slot)
        image = res + jnp.where(col < L, dot(pick[...], mz[slot].reshape(256, 256)), 0.0)
        ring_wait(sz, vs, vq, slot)
        ring = jnp.sum(sz[slot], axis=0)
        norm = jnp.sum(jnp.where(lane1 < 64, plane, 0.0), axis=1, keepdims=True)
        bend = norm + jnp.sum(jnp.where(lane1 >= 64, ring, 0.0), axis=1, keepdims=True)
        first = i == 0
        ratio = jnp.where(first, 0.0, norm / norm_old)
        step = norm / (bend - jnp.where(first, 0.0, ratio * norm / step_old))
        turned = image + ratio * s[...]
        s[...] = turned
        ahead = res + ratio * p[...]
        p[...] = ahead
        x[...] = x[...] + step * ahead
        r[...] = res - step * turned
        return norm, step

    one = jnp.ones((1, 1), F32)
    lax.fori_loop(0, ITERS, iteration, (one, one))

    hi, lo = halves(x[...])
    grown = dot(hi, sh[...]) + dot(lo, sh[...]) + dot(hi, sl[...])
    out[:, 0:8, :] = grown.astype(BF16).reshape(NM, 8, 256)
    out[:, 8:16, :] = r[...].astype(BF16).reshape(NM, 8, 256)

    def give(t, carry):
        m = (my_m + t) % NM
        pltpu.make_async_remote_copy(
            src_ref=out.at[m // NCH * NZ + my_z], dst_ref=got.at[my_m],
            send_sem=os.at[m], recv_sem=oq.at[my_m],
            device_id=plane_peer(m), device_id_type=MESH).start()
        return carry

    lax.fori_loop(1, NM, give, 0)
    got[my_m] = out[my_y * NZ + my_z]

    def take(t, carry):
        m = (my_m + t) % NM
        pltpu.make_async_remote_copy(
            src_ref=out.at[m // NCH * NZ + my_z], dst_ref=got.at[m],
            send_sem=os.at[m], recv_sem=oq.at[m],
            device_id=plane_peer(m), device_id_type=MESH).wait()
        return carry

    lax.fori_loop(1, NM, take, 0)
    for k, ref in ((0, inc_ref), (1, res_ref)):
        rows = got[:, 8 * k: 8 * k + 8, :].reshape(256, 256)
        flat = dot_t(eye[...], rows).astype(BF16)
        ref[...] = dot(flat, perm[...])[0:L]


def per_device(jacobian, departures, obs_weights, column_count, grid_block, sqrt_cov):
    jt = jnp.transpose(jacobian, (2, 1, 0))
    vmem = pl.BlockSpec(memory_space=pltpu.VMEM)
    smem = pl.BlockSpec(memory_space=pltpu.SMEM)
    dma = pltpu.SemaphoreType.DMA
    inc, res = pl.pallas_call(
        kernel,
        out_shape=(jax.ShapeDtypeStruct((L, 256), F32),) * 2,
        in_specs=[smem, smem, vmem, vmem, vmem, vmem],
        out_specs=(vmem, vmem),
        scratch_shapes=[
            pltpu.VMEM((NM, 8, WIDE), BF16),
            pltpu.VMEM((NM, 8, WIDE), BF16),
            pltpu.VMEM((NM, 8, 128), F32),
            pltpu.VMEM((NM, 8, 128), F32),
            pltpu.VMEM((8, WIDE), F32),
            pltpu.VMEM((NM, 8, 128), F32),
            pltpu.VMEM((NY, 8, 256), F32),
            pltpu.VMEM((256, 256), BF16),
            pltpu.VMEM((256, 256), BF16),
            pltpu.VMEM((256, 256), BF16),
            pltpu.VMEM((256, 256), BF16),
            pltpu.VMEM((32, 256), F32),
            pltpu.VMEM((256, 256), BF16),
            pltpu.VMEM((NY, 8, 128), F32),
            pltpu.VMEM((256, 256), F32),
            pltpu.VMEM((256, 256), F32),
            pltpu.VMEM((256, 256), F32),
            pltpu.VMEM((256, 256), F32),
            pltpu.VMEM((2, NZ, 32, 256), BF16),
            pltpu.VMEM((2, NM, 1, 128), F32),
            pltpu.VMEM((2, NZ, 1, 128), F32),
            pltpu.VMEM((NM, 16, 256), BF16),
            pltpu.VMEM((NM, 16, 256), BF16),
            dma((NM,)), dma((NM,)),
            dma((2, NZ)), dma((2, NZ)),
            dma((2, NM)), dma((2, NM)),
            dma((2, NZ)), dma((2, NZ)),
            dma((NY,)), dma((NY,)),
            dma((NM,)), dma((NM,)),
        ],
        compiler_params=pltpu.CompilerParams(
            collective_id=0, has_side_effects=True, vmem_limit_bytes=50 * 1024 * 1024),
        name="cg",
    )(column_count, grid_block, jt, obs_weights, departures, sqrt_cov)
    return inc.T, res.T


def solution(mesh):
    split = Mesh(mesh.devices.reshape(NY, NZ, NX, NC), ("obs_0", "obs_1", "chan_0", "chan_1"))
    return jax.shard_map(
        per_device,
        mesh=split,
        in_specs=(P(OBS, CHAN, None), P(CHAN, OBS), P(CHAN, OBS), P(OBS), P(OBS), P()),
        out_specs=(P(OBS, None), P(OBS, None)),
        check_vma=False,
    )
```

time: 735 us -> 128 us (0.17)
  blocking collectives: 626 us -> 0 us
  Pallas kernels: 0 us -> 121 us
  starting transfers between devices: 23.8 us -> 0 us
  waiting for transfers between devices: 19.1 us -> 0 us
  other arithmetic: 14.7 us -> 0 us
  local copies, waits for them, and re-layouts: 20.6 us -> 6.03 us
  between operations: 14.3 us -> 1.3 us
  matrix products: 10.7 us -> 0 us
    psum x36 -> x0, blocking collectives: 356 us -> none  [one_axis_at_a_time(): return functools.reduce(lax.psum, axes, value)]
    all_to_all x20 -> x0, blocking collectives: 257 us -> none  [the longest x5 83.6 us: per_device(): lax.all_to_all(to_outgoing.reshape(obs_count, share_cols, layers), OBS, s...]
    pallas_call x0 -> x1, Pallas kernels: none -> 121 us  [per_device(): pl.pallas_call(kernel, out_shape=(jax.ShapeDtypeStruct((L, 256), F32),) *...]
    all_to_all x3 -> x0, starting transfers between devices: 23.8 us -> none  [the longest x1 12 us: from_everyone(): return lax.all_to_all(copies, axis, split_axis=0, concat_axis=0, tiled=True)]
    all_to_all x3 -> x0, waiting for transfers between devices: 19.1 us -> none  [the longest x1 9.61 us: to_owners(): lax.all_to_all(outgoing.reshape(obs_count, share_cols, layers), OBS, spli...]
    all_gather x1 -> x0, blocking collectives: 13 us -> none  [side_by_side(): whole = lax.all_gather(both, axis, axis=dim, tiled=True)]
    dot_general x34 -> x0, matrix products: 10.7 us -> none  [the longest x6 4.57 us: spread_back(): lax.dot_general(field.reshape(-1, layers), sqrt_cov, (((1,), (1,)), ((),...]
    reshape x31 -> x0, local copies, waits for them, and re-layouts: 9.31 us -> none  [the longest x5 3.69 us: per_device(): to_outgoing.reshape(obs_count, share_cols, layers)]
  transfers between devices with their start and end apart: 3 -> 0, of which waited for: 3 -> 0; matrix products, arithmetic and copies ran while one was open for 1% -> 0% of each run, Pallas kernels for 0% -> 0%
where the time goes in v1:
time: 128 us
  Pallas kernels  121 us (95%)
  local copies, waits for them, and re-layouts  6.03 us (5%)
  between operations  1.3 us (1%)
    pallas_call x1, Pallas kernels, per_device(): pl.pallas_call(kernel, out_shape=(jax.ShapeDtypeStruct((L, 256), F32),) *...  121 us
    unnamed x12, local copies, waits for them, and re-layouts  6.03 us

profile of v1, /device:TPU:1, one launch (start us, length us, event | category | flops | bytes accessed | tf_op | source)
XLA Modules:
  0.0 127.9 jit_solution(15985904122178793645)
XLA Ops:
  1.3 0.0 copy-start
  1.3 1.6 %copy-done = bf16[256,32,137]{0,1,2:T(8,128)(2,1)S(1)} copy-done((bf16[256,32,137]{0,1,2:T(8,128)(2,1)S(1)}, bf16[256,32,137]{0,1,2:T(8,128)(2,1)}, u32[]{:S(2)}) %copy-start) | copy-done | bytes 2244632
  2.9 0.0 copy-start.1
  2.9 0.9 copy-done.1
  3.8 0.0 copy-start.2
  3.8 0.8 copy-done.2
  4.6 0.0 copy-start.3
  4.6 0.8 copy-done.3
  5.3 0.0 copy-start.4
  5.3 0.7 copy-done.4
  6.0 120.6 %cg.1 = (f32[137,256]{1,0:T(8,128)S(1)}, f32[137,256]{1,0:T(8,128)S(1)}) custom-call(s32[1]{0:T(128)S(6)} %copy.10.cnt_ref, s32[2]{0:T(128)S(1)} %copy-done.4, bf16[137,32,256]{2,1,0:T(8,128)(2,1)S(1)} %bitcast.3, f32[32,256]{1,0:T(8,128)S(1)} %copy-done.2, f32[32,256]{1,0:T(8,128)S(1)} %copy-done.3, f32[137,137]{1,0:T(8,128)S(1)} %copy-done.1), custom_call_target="tpu_custom_call" | custom-call | tf_op jit(solution)/shard_map/cg/pallas_call | solution.py:363
  126.6 0.7 copy.11
  127.2 0.7 copy.12
Async XLA Ops:
  1.3 1.6 %copy-start = (bf16[256,32,137]{0,1,2:T(8,128)(2,1)S(1)}, bf16[256,32,137]{0,1,2:T(8,128)(2,1)}, u32[]{:S(2)}) copy-start(bf16[256,32,137]{0,1,2:T(8,128)(2,1)} %param.6) | copy-start | bytes 6733828
  2.9 0.9 copy-start.1
  3.8 0.8 copy-start.2
  4.6 0.8 copy-start.3
  5.3 0.7 copy-start.4

commit v2 on v1

v2 whole, which is shorter than its diff:
```python
import jax
import jax.numpy as jnp
from jax import lax
from jax.experimental import pallas as pl
from jax.experimental.pallas import tpu as pltpu
from jax.sharding import Mesh
from jax.sharding import PartitionSpec as P

ITERS = 5
L = 137
NY, NZ, NX, NC = 4, 8, 4, 2
NCH = NX * NC
NM = NY * NCH
LH = 35
CHUNKS = 5
PER = LH // CHUNKS
WIDE = LH * 128
ID_LANE = 16
OBS = ("obs_0", "obs_1")
CHAN = ("chan_0", "chan_1")
MESH = pl.DeviceIdType.MESH
F32 = jnp.float32
BF16 = jnp.bfloat16


def iota(shape, dim):
    return lax.broadcasted_iota(jnp.int32, shape, dim)


def dot(a, b):
    return jnp.dot(a, b, preferred_element_type=F32)


def dot_t(a, b):
    return lax.dot_general(a, b, (((1,), (1,)), ((), ())), preferred_element_type=F32)


def halves(v):
    hi = v.astype(BF16)
    return hi, (v - hi.astype(F32)).astype(BF16)


def lanes(q):
    return pl.ds(q * 128, 128)


def kernel(
    cnt_hbm, gb_hbm, jt_hbm, w_hbm, d_hbm, s_hbm,
    inc_ref, res_ref,
    cnt_ref, gb_ref, jv, w_ref, d_ref, s_ref,
    sb, jr, mw, fx, sv, ts, sh, sl, perm, eye, spot, own, pick, ids, tt, so, sr, cm,
    r, p, s, x, w, v, mz, sx, out, got,
    fs, js, jq, as_, aq, zs, zq, xs, xq, ys, yq, os, oq,
):
    my_y = lax.axis_index("obs_0")
    my_z = lax.axis_index("obs_1")
    my_x = lax.axis_index("chan_0")
    my_c = lax.axis_index("chan_1")
    my_m = my_y * NCH + my_x * NC + my_c

    fetches = [
        pltpu.make_async_copy(a, b, fs.at[k])
        for k, (a, b) in enumerate((
            (w_hbm, w_ref), (d_hbm, d_ref), (cnt_hbm, cnt_ref), (gb_hbm, gb_ref), (s_hbm, s_ref)))
    ]
    blocks = []
    for q in range(CHUNKS):
        first, last = 4 * PER * q, min(4 * PER * (q + 1), L)
        blocks.append(pltpu.make_async_copy(
            jt_hbm.at[first:last], jv.at[first:last], fs.at[len(fetches) + q]))
    for copy in (blocks[0], *fetches, *blocks[1:]):
        copy.start()

    def plane_peer(m):
        return (m // NCH, my_z, (m % NCH) // NC, m % NC)

    def ring_peer(z):
        return (my_y, z, my_x, my_c)

    barrier = pltpu.get_barrier_semaphore()

    def greet_plane(t, carry):
        pl.semaphore_signal(barrier, inc=1, device_id=plane_peer((my_m + t) % NM), device_id_type=MESH)
        return carry

    def greet_ring(t, carry):
        pl.semaphore_signal(barrier, inc=1, device_id=ring_peer((my_z + t) % NZ), device_id_type=MESH)
        return carry

    lax.fori_loop(1, NM, greet_plane, 0)
    lax.fori_loop(1, NZ, greet_ring, 0)

    row = iota((256, 256), 0)
    col = iota((256, 256), 1)
    lane = iota((8, 128), 1)
    lane1 = iota((1, 128), 1)
    perm[...] = jnp.where(
        ((row & 4) << 5) + ((row >> 3) << 2) + (row & 3) == col, 1.0, 0.0).astype(BF16)
    jv[L:144] = jnp.zeros((144 - L, 32, 256), BF16)

    def turn(h, carry):
        block = jv[pl.ds(4 * h, 4)].reshape(128, 256)
        turned = dot_t(perm[...], block).astype(BF16)
        sb[:, :, pl.ds(pl.multiple_of(h * 128, 128), 128)] = turned.reshape(NM, 8, 128)
        return carry

    def send_chunk(q):
        def send(t, carry):
            m = (my_m + t) % NM
            part = pl.ds(q * PER * 128, PER * 128)
            pltpu.make_async_remote_copy(
                src_ref=sb.at[m, :, part], dst_ref=jr.at[my_m, :, part],
                send_sem=js.at[m], recv_sem=jq.at[my_m],
                device_id=plane_peer(m), device_id_type=MESH).start()
            return carry

        lax.fori_loop(1, NM, send, 0)

    blocks[0].wait()
    lax.fori_loop(0, PER, turn, 0, unroll=True)
    pl.semaphore_wait(barrier, NM - 1 + NZ - 1)
    send_chunk(0)

    for copy in fetches:
        copy.wait()
    sh[...] = jnp.zeros_like(sh)
    sl[...] = jnp.zeros_like(sl)
    root_hi, root_lo = halves(s_ref[...])
    sh[0:L, 0:L] = root_hi
    sl[0:L, 0:L] = root_lo
    r4 = iota((8, 128), 0)
    ids[my_y] = jnp.where(r4 < 4, gb_ref[0], gb_ref[1]).astype(F32)

    def id_copy(t, arriving):
        peer = (my_y + t) % NY
        at = peer if arriving else my_y
        return pltpu.make_async_remote_copy(
            src_ref=ids.at[at], dst_ref=ids.at[at], send_sem=ys.at[t], recv_sem=yq.at[at],
            device_id=(peer, my_z, my_x, my_c), device_id_type=MESH)

    for t in range(1, NY):
        id_copy(t, False).start()

    mask = jnp.where(iota((32, 256), 1) < cnt_ref[0], 1.0, 0.0)
    weight = mask * w_ref[...]
    weight_hi, weight_lo = halves(weight)
    scaled_d = (weight * d_ref[...]).astype(BF16)
    d_ref[...] = scaled_d.astype(F32)

    for copy in blocks[1:]:
        copy.wait()

    def gather_source(g, carry):
        part = jv[pl.ds(8 * g, 8)].astype(F32) * d_ref[...][None]
        tt[pl.ds(pl.multiple_of(8 * g, 8), 8), :] = jnp.sum(part, axis=1)
        return carry

    lax.fori_loop(0, 18, gather_source, 0, unroll=2)
    hi, lo = halves(tt[...])
    flat = dot_t(perm[...], hi) + dot_t(perm[...], lo)
    hi, lo = halves(flat)
    front = sh[:, 0:144]
    flat = dot_t(hi, front) + dot_t(lo, front) + dot_t(hi, sl[:, 0:144])
    so[...] = flat.astype(BF16).reshape(NM, 8, 256)

    def source_copy(t, arriving):
        m = (my_m + t) % NM
        return pltpu.make_async_remote_copy(
            src_ref=so.at[m], dst_ref=sr.at[m if arriving else my_m],
            send_sem=as_.at[m], recv_sem=aq.at[m if arriving else my_m],
            device_id=plane_peer(m), device_id_type=MESH)

    def source_send(t, carry):
        source_copy(t, False).start()
        return carry

    lax.fori_loop(1, NM, source_send, 0)
    sr[my_m] = so[my_m]

    for q in range(1, CHUNKS):
        if q < CHUNKS - 1:
            lax.fori_loop(q * PER, (q + 1) * PER, turn, 0, unroll=True)
        else:
            lax.fori_loop(q * PER, (q + 1) * PER - 1, turn, 0, unroll=True)
            block = jnp.concatenate([jv[L - 1], weight_hi, weight_lo, jnp.zeros_like(weight_hi)], axis=0)
            turned = dot_t(perm[...], block).astype(BF16)
            sb[:, :, lanes(LH - 1)] = turned.reshape(NM, 8, 128)
        send_chunk(q)
    jr[my_m] = sb[my_m]

    eye[...] = jnp.where(row == col, 1.0, 0.0).astype(BF16)
    spot[...] = jnp.where(
        iota((128, 128), 0) >> 5 == (iota((128, 128), 1) & 3), 1.0, 0.0).astype(BF16)
    for t in range(1, NY):
        id_copy(t, True).wait()
    row2 = iota((8, 256), 0)
    lane2 = iota((8, 256), 1)
    for y in range(NY):
        ident = ids[y][:, 0:1].astype(jnp.int32)
        own[pl.ds(8 * y, 8), :] = jnp.where(
            (ident == lane2 >> 2) & ((row2 & 3) == (lane2 & 3)), 1.0, 0.0)

    def source_wait(t, carry):
        source_copy(t, True).wait()
        return carry

    def ring_copy(slot, t, arriving):
        z = (my_z + t) % NZ
        at = z if arriving else my_z
        return pltpu.make_async_remote_copy(
            src_ref=mz.at[slot, at], dst_ref=mz.at[slot, at],
            send_sem=zs.at[slot, t], recv_sem=zq.at[slot, at],
            device_id=ring_peer(z), device_id_type=MESH)

    def ring_send(slot, value):
        mz[slot, my_z, 0:32] = value[:, :, 0:128].reshape(32, 128)
        packed = None
        for y in range(NY):
            part = jnp.where(lane == ID_LANE, ids[y], value[y, :, 128:256])
            part = pltpu.roll(part, 32 * y, 1) if y else part
            packed = part if packed is None else packed + part
        mz[slot, my_z, 32:40] = packed
        for t in (4, 3, 5, 2, 6, 1, 7):
            ring_copy(slot, t, False).start()

    def ring_wait(slot):
        for t in range(1, NZ):
            ring_copy(slot, t, True).wait()
        for z in range(NZ):
            cm[32 * z: 32 * z + 32, 0:128] = mz[slot, z, 0:32]
            packed = mz[slot, z, 32:40]
            for y in range(NY):
                at = 32 * z + 8 * y
                cm[at: at + 8, 128:256] = pltpu.roll(packed, 128 - 32 * y, 1) if y else packed

    def collect():
        hi, lo = halves(cm[...])
        return jnp.where(col < L, dot(pick[...], hi) + dot(pick[...], lo), 0.0)

    lax.fori_loop(1, NM, source_wait, 0)
    ring_send(0, jnp.sum(sr[...].astype(F32).reshape(NY, NCH, 8, 256), axis=1))
    ring_wait(0)
    ident = cm[:, 128 + ID_LANE: 128 + ID_LANE + 1].astype(jnp.int32)
    match = jnp.where((ident == col >> 2) & ((row & 3) == (col & 3)), 1.0, 0.0).astype(BF16)
    pick[...] = dot_t(eye[...], match).astype(BF16)
    r[...] = collect()

    def across(a):
        a = a + pltpu.roll(a, 64, 1)
        return a + pltpu.roll(a, 32, 1)

    def spread_near(grid):
        hi, lo = halves(grid)
        choose = own[...].astype(BF16)
        near_hi = dot(choose, hi).astype(BF16)
        near_lo = dot(choose, lo).astype(BF16)
        field = dot(near_hi, sh[...]) + dot(near_lo, sh[...]) + dot(near_hi, sl[...])
        ts[...] = field.reshape(NY, 8, 256)

    def widen(y):
        for h in range(LH):
            base = ts[y, :, 0:128] if h < 32 else ts[y, :, 128:256]
            fx[y, :, lanes(h)] = jnp.take_along_axis(base, 4 * (h % 32) + (lane >> 5), axis=1)

    def predict_one(m, y):
        parts = [None] * 4
        for h in range(LH):
            prod = jr[m, :, lanes(h)].astype(F32) * fx[y, :, lanes(h)]
            parts[h % 4] = prod if parts[h % 4] is None else parts[h % 4] + prod
        return across((parts[0] + parts[1]) + (parts[2] + parts[3]))

    def terms(slot):
        def group(y, carry):
            acc = []
            for h in range(LH):
                total = None
                for c in range(NCH):
                    prod = jr[y * NCH + c, :, lanes(h)].astype(F32) * sv[y * NCH + c]
                    total = prod if total is None else total + prod
                acc.append(total)
            hi, lo = halves(jnp.concatenate(acc, axis=0))
            sums = dot(hi, spot[...]) + dot(lo, spot[...])
            first = jnp.zeros((8, 128), F32)
            second = jnp.zeros((8, 128), F32)
            for h in range(LH):
                piece = jnp.where(lane >> 2 == h % 32, sums[8 * h: 8 * h + 8], 0.0)
                if h < 32:
                    first = first + piece
                else:
                    second = second + piece
            ts[y, :, 0:128] = first
            ts[y, :, 128:256] = second
            return carry

        lax.fori_loop(0, NY, group, 0)
        hi, lo = halves(ts[...].reshape(32, 256))
        back = dot_t(hi, sh[...]) + dot_t(lo, sh[...]) + dot_t(hi, sl[...])
        ring_send(slot, back.reshape(NY, 8, 256))

    spread_near(r[...])

    def widen_group(y, carry):
        widen(y)
        return carry

    lax.fori_loop(0, NY, widen_group, 0)

    def first_predict(m):
        extra = jr[m, :, lanes(LH - 1)].astype(F32)
        weights = across(jnp.where((lane >= 32) & (lane < 96), extra, 0.0))
        mw[m] = weights
        sv[m] = weights * predict_one(m, m // NCH)

    first_predict(my_m)

    def arrive(t, carry):
        m = (my_m + NM - t) % NM
        pltpu.make_async_remote_copy(
            src_ref=sb.at[m], dst_ref=jr.at[m], send_sem=js.at[m], recv_sem=jq.at[m],
            device_id=plane_peer(m), device_id_type=MESH).wait()
        first_predict(m)
        return carry

    lax.fori_loop(1, NM, arrive, 0)
    terms(1)
    p[...] = jnp.zeros_like(p)
    s[...] = jnp.zeros_like(s)
    x[...] = jnp.zeros_like(x)
    v[...] = jnp.zeros_like(v)
    ring_wait(1)
    w[...] = r[...] + collect()

    def plane_copy(slot, t, arriving):
        m = (my_m + t) % NM
        at = m if arriving else my_m
        return pltpu.make_async_remote_copy(
            src_ref=sx.at[slot, at], dst_ref=sx.at[slot, at],
            send_sem=xs.at[slot, m], recv_sem=xq.at[slot, at],
            device_id=plane_peer(m), device_id_type=MESH)

    def scalars_send(slot):
        res = r[...]
        norm = jnp.sum(res * res, axis=0, keepdims=True)
        norm = norm[:, 0:128] + norm[:, 128:256]
        bend = jnp.sum(res * w[...], axis=0, keepdims=True)
        bend = bend[:, 0:128] + bend[:, 128:256]
        sx[slot, my_m] = jnp.where(
            lane1 < 64, norm + pltpu.roll(norm, 64, 1), bend + pltpu.roll(bend, 64, 1))

        def start(t, carry):
            plane_copy(slot, t, False).start()
            return carry

        lax.fori_loop(1, NM, start, 0)

    def advance(i, slot, norm_old, step_old):
        def finish(t, carry):
            plane_copy(slot, t, True).wait()
            return carry

        lax.fori_loop(1, NM, finish, 0)
        both = jnp.sum(sx[slot], axis=0)
        norm = jnp.sum(jnp.where(lane1 < 64, both, 0.0), axis=1, keepdims=True)
        bend = jnp.sum(jnp.where(lane1 < 64, 0.0, both), axis=1, keepdims=True)
        ratio = jnp.where(i == 0, 0.0, norm / norm_old)
        step = norm / (bend - jnp.where(i == 0, 0.0, ratio * norm / step_old))
        turned = w[...] + ratio * s[...]
        s[...] = turned
        ahead = r[...] + ratio * p[...]
        p[...] = ahead
        x[...] = x[...] + step * ahead
        r[...] = r[...] - step * turned
        return norm, step, ratio

    def iteration(i, carry):
        slot = i & 1
        spread_near(w[...])
        scalars_send(slot)

        def predict(y, carry):
            widen(y)
            for c in range(NCH):
                m = y * NCH + c
                sv[m] = mw[m] * predict_one(m, y)
            return carry

        lax.fori_loop(0, NY, predict, 0)
        terms(slot)
        norm, step, ratio = advance(i, slot, *carry)
        ring_wait(slot)
        along = w[...] + collect() + ratio * v[...]
        v[...] = along
        w[...] = w[...] - step * along
        return norm, step

    one = jnp.ones((1, 1), F32)
    norm, step = lax.fori_loop(0, ITERS - 1, iteration, (one, one))
    scalars_send((ITERS - 1) & 1)
    advance(ITERS - 1, (ITERS - 1) & 1, norm, step)

    hi, lo = halves(x[...])
    grown = dot(hi, sh[...]) + dot(lo, sh[...]) + dot(hi, sl[...])
    out[:, 0:8, :] = grown.astype(BF16).reshape(NM, 8, 256)
    out[:, 8:16, :] = r[...].astype(BF16).reshape(NM, 8, 256)

    def result_copy(t, arriving):
        m = (my_m + t) % NM
        at = m if arriving else my_m
        return pltpu.make_async_remote_copy(
            src_ref=out.at[m // NCH * NZ + my_z], dst_ref=got.at[at],
            send_sem=os.at[m], recv_sem=oq.at[at],
            device_id=plane_peer(m), device_id_type=MESH)

    def give(t, carry):
        result_copy(t, False).start()
        return carry

    def take(t, carry):
        result_copy(t, True).wait()
        return carry

    lax.fori_loop(1, NM, give, 0)
    got[my_m] = out[my_y * NZ + my_z]
    lax.fori_loop(1, NM, take, 0)
    for k, ref in ((0, inc_ref), (1, res_ref)):
        rows = got[:, 8 * k: 8 * k + 8, :].reshape(256, 256)
        flat = dot_t(eye[0:144, :], rows).astype(BF16)
        ref[...] = dot(flat, perm[...])[0:L]


def per_device(jacobian, departures, obs_weights, column_count, grid_block, sqrt_cov):
    jt = jnp.transpose(jacobian, (2, 1, 0))
    vmem = pl.BlockSpec(memory_space=pltpu.VMEM)
    dma = pltpu.SemaphoreType.DMA
    state = pltpu.VMEM((256, 256), F32)
    table = pltpu.VMEM((256, 256), BF16)
    inc, res = pl.pallas_call(
        kernel,
        out_shape=(jax.ShapeDtypeStruct((L, 256), F32),) * 2,
        in_specs=[pl.BlockSpec(memory_space=pltpu.HBM)] * 6,
        out_specs=(vmem, vmem),
        scratch_shapes=[
            pltpu.SMEM((1,), jnp.int32),
            pltpu.SMEM((2,), jnp.int32),
            pltpu.VMEM((144, 32, 256), BF16),
            pltpu.VMEM((32, 256), F32),
            pltpu.VMEM((32, 256), F32),
            pltpu.VMEM((L, L), F32),
            pltpu.VMEM((NM, 8, WIDE), BF16),
            pltpu.VMEM((NM, 8, WIDE), BF16),
            pltpu.VMEM((NM, 8, 128), F32),
            pltpu.VMEM((NY, 8, WIDE), F32),
            pltpu.VMEM((NM, 8, 128), F32),
            pltpu.VMEM((NY, 8, 256), F32),
            table, table, table, table,
            pltpu.VMEM((128, 128), BF16),
            pltpu.VMEM((32, 256), F32),
            table,
            pltpu.VMEM((NY, 8, 128), F32),
            pltpu.VMEM((144, 256), F32),
            pltpu.VMEM((NM, 8, 256), BF16),
            pltpu.VMEM((NM, 8, 256), BF16),
            state,
            state, state, state, state, state, state,
            pltpu.VMEM((2, NZ, 40, 128), F32),
            pltpu.VMEM((2, NM, 1, 128), F32),
            pltpu.VMEM((NM, 16, 256), BF16),
            pltpu.VMEM((NM, 16, 256), BF16),
            dma((5 + CHUNKS,)),
            dma((NM,)), dma((NM,)),
            dma((NM,)), dma((NM,)),
            dma((2, NZ)), dma((2, NZ)),
            dma((2, NM)), dma((2, NM)),
            dma((NY,)), dma((NY,)),
            dma((NM,)), dma((NM,)),
        ],
        compiler_params=pltpu.CompilerParams(
            collective_id=0, has_side_effects=True, vmem_limit_bytes=67_000_000),
        name="cg",
    )(column_count, grid_block, jt, obs_weights, departures, sqrt_cov)
    return inc.T, res.T


def solution(mesh):
    split = Mesh(mesh.devices.reshape(NY, NZ, NX, NC), ("obs_0", "obs_1", "chan_0", "chan_1"))
    return jax.shard_map(
        per_device,
        mesh=split,
        in_specs=(P(OBS, CHAN, None), P(CHAN, OBS), P(CHAN, OBS), P(OBS), P(OBS), P()),
        out_specs=(P(OBS, None), P(OBS, None)),
        check_vma=False,
    )
```

time: 128 us -> 112 us (0.88)
  Pallas kernels: 121 us -> 108 us
  local copies, waits for them, and re-layouts: 6.03 us -> 3.16 us
    pallas_call x1, Pallas kernels: 121 us -> 108 us  [per_device(): pl.pallas_call(kernel, out_shape=(jax.ShapeDtypeStruct((L, 256), F32),) *...]
    unnamed x12 -> x2, local copies, waits for them, and re-layouts: 6.03 us -> 3.16 us
where the time goes in v2:
time: 112 us
  Pallas kernels  108 us (96%)
  local copies, waits for them, and re-layouts  3.16 us (3%)
  between operations  1.29 us (1%)
    pallas_call x1, Pallas kernels, per_device(): pl.pallas_call(kernel, out_shape=(jax.ShapeDtypeStruct((L, 256), F32),) *...  108 us
    unnamed x2, local copies, waits for them, and re-layouts  3.16 us

profile of v2, /device:TPU:1, one launch (start us, length us, event | category | flops | bytes accessed | tf_op | source)
XLA Modules:
  0.0 112.0 jit_solution(8021973576662644113)
XLA Ops:
  1.3 107.6 %cg.1 = (f32[137,256]{1,0:T(8,128)}, f32[137,256]{1,0:T(8,128)}) custom-call(s32[1]{0:T(128)S(6)} %copy.10.cnt_hbm, s32[2]{0:T(128)} %gb_hbm.1, bf16[137,32,256]{2,1,0:T(8,128)(2,1)} %bitcast.3, f32[32,256]{1,0:T(8,128)} %w_hbm.1, f32[32,256]{1,0:T(8,128)} %d_hbm.1, f32[137,137]{1,0:T(8,128)} %s_hbm.1), custom_call_target="tpu_custom_call" | custom-call | tf_op jit(solution)/shard_map/cg/pallas_call | solution.py:437
  108.9 1.6 %copy.11 = f32[256,137]{0,1:T(8,128)} copy(f32[256,137]{0,1:T(8,128)} %bitcast.5) | data formatting | bytes 280576
  110.4 1.6 %copy.12 = f32[256,137]{0,1:T(8,128)} copy(f32[256,137]{0,1:T(8,128)} %bitcast.4) | data formatting | bytes 280576

commit v3 on v2

--- a/solution.py
+++ b/solution.py
@@ -48,8 +48,8 @@
     cnt_hbm, gb_hbm, jt_hbm, w_hbm, d_hbm, s_hbm,
     inc_ref, res_ref,
     cnt_ref, gb_ref, jv, w_ref, d_ref, s_ref,
-    sb, jr, mw, fx, sv, ts, sh, sl, perm, eye, spot, own, pick, ids, tt, so, sr, cm,
-    r, p, s, x, w, v, mz, sx, out, got,
+    sb, jr, jf, mw, fx, sv, ff, fv, sh, sl, qh, ql, perm, eye, spot, own, near, pick, ids, tt, so, sr, cm,
+    r, p, s, x, w, v, g, mz, sx, out, got,
     fs, js, jq, as_, aq, zs, zq, xs, xq, ys, yq, os, oq,
 ):
     my_y = lax.axis_index("obs_0")
@@ -104,10 +104,11 @@
         sb[:, :, pl.ds(pl.multiple_of(h * 128, 128), 128)] = turned.reshape(NM, 8, 128)
         return carry
 
-    def send_chunk(q):
+    def send_part(first, last):
+        part = pl.ds(first * 128, (last - first) * 128)
+
         def send(t, carry):
             m = (my_m + t) % NM
-            part = pl.ds(q * PER * 128, PER * 128)
             pltpu.make_async_remote_copy(
                 src_ref=sb.at[m, :, part], dst_ref=jr.at[my_m, :, part],
                 send_sem=js.at[m], recv_sem=jq.at[my_m],
@@ -119,7 +120,7 @@
     blocks[0].wait()
     lax.fori_loop(0, PER, turn, 0, unroll=True)
     pl.semaphore_wait(barrier, NM - 1 + NZ - 1)
-    send_chunk(0)
+    send_part(0, PER)
 
     for copy in fetches:
         copy.wait()
@@ -158,10 +159,7 @@
     lax.fori_loop(0, 18, gather_source, 0, unroll=2)
     hi, lo = halves(tt[...])
     flat = dot_t(perm[...], hi) + dot_t(perm[...], lo)
-    hi, lo = halves(flat)
-    front = sh[:, 0:144]
-    flat = dot_t(hi, front) + dot_t(lo, front) + dot_t(hi, sl[:, 0:144])
-    so[...] = flat.astype(BF16).reshape(NM, 8, 256)
+    so[...] = jnp.pad(flat, ((0, 0), (0, 112))).astype(BF16).reshape(NM, 8, 256)
 
     def source_copy(t, arriving):
         m = (my_m + t) % NM
@@ -177,20 +175,19 @@
     lax.fori_loop(1, NM, source_send, 0)
     sr[my_m] = so[my_m]
 
-    for q in range(1, CHUNKS):
-        if q < CHUNKS - 1:
-            lax.fori_loop(q * PER, (q + 1) * PER, turn, 0, unroll=True)
-        else:
-            lax.fori_loop(q * PER, (q + 1) * PER - 1, turn, 0, unroll=True)
-            block = jnp.concatenate([jv[L - 1], weight_hi, weight_lo, jnp.zeros_like(weight_hi)], axis=0)
-            turned = dot_t(perm[...], block).astype(BF16)
-            sb[:, :, lanes(LH - 1)] = turned.reshape(NM, 8, 128)
-        send_chunk(q)
+    lax.fori_loop(PER, LH - 1, turn, 0, unroll=9)
+    block = jnp.concatenate([jv[L - 1], weight_hi, weight_lo, jnp.zeros_like(weight_hi)], axis=0)
+    sb[:, :, lanes(LH - 1)] = dot_t(perm[...], block).astype(BF16).reshape(NM, 8, 128)
+    send_part(PER, LH)
     jr[my_m] = sb[my_m]
 
     eye[...] = jnp.where(row == col, 1.0, 0.0).astype(BF16)
     spot[...] = jnp.where(
         iota((128, 128), 0) >> 5 == (iota((128, 128), 1) & 3), 1.0, 0.0).astype(BF16)
+    turned_hi = dot_t(eye[...], sh[...]).astype(BF16)
+    turned_lo = dot_t(eye[...], sl[...]).astype(BF16)
+    square = dot(turned_hi, sh[...]) + dot(turned_lo, sh[...]) + dot(turned_hi, sl[...])
+    qh[...], ql[...] = halves(square)
     for t in range(1, NY):
         id_copy(t, True).wait()
     row2 = iota((8, 256), 0)
@@ -212,16 +209,21 @@
             send_sem=zs.at[slot, t], recv_sem=zq.at[slot, at],
             device_id=ring_peer(z), device_id_type=MESH)
 
-    def ring_send(slot, value):
-        mz[slot, my_z, 0:32] = value[:, :, 0:128].reshape(32, 128)
+    def ring_start(slot, part):
+        for t in (4, 3, 5, 2, 6, 1, 7):
+            pltpu.make_async_remote_copy(
+                src_ref=mz.at[slot, my_z, part], dst_ref=mz.at[slot, my_z, part],
+                send_sem=zs.at[slot, t], recv_sem=zq.at[slot, my_z],
+                device_id=ring_peer((my_z + t) % NZ), device_id_type=MESH).start()
+
+    def ring_tail(slot, tails):
         packed = None
         for y in range(NY):
-            part = jnp.where(lane == ID_LANE, ids[y], value[y, :, 128:256])
+            part = jnp.where(lane == ID_LANE, ids[y], tails[y])
             part = pltpu.roll(part, 32 * y, 1) if y else part
             packed = part if packed is None else packed + part
         mz[slot, my_z, 32:40] = packed
-        for t in (4, 3, 5, 2, 6, 1, 7):
-            ring_copy(slot, t, False).start()
+        ring_start(slot, pl.ds(32, 8))
 
     def ring_wait(slot):
         for t in range(1, NZ):
@@ -233,71 +235,64 @@
                 at = 32 * z + 8 * y
                 cm[at: at + 8, 128:256] = pltpu.roll(packed, 128 - 32 * y, 1) if y else packed
 
+    def times(a, hi_ref, lo_ref):
+        hi, lo = halves(a)
+        return dot(hi, hi_ref[...]) + dot(lo, hi_ref[...]) + dot(hi, lo_ref[...])
+
     def collect():
         hi, lo = halves(cm[...])
-        return jnp.where(col < L, dot(pick[...], hi) + dot(pick[...], lo), 0.0)
+        close = times(dot(near[...], hi) + dot(near[...], lo), qh, ql)
+        hi, lo = halves(dot(pick[...], hi) + dot(pick[...], lo))
+        return dot_t(hi, sh[...]) + dot_t(lo, sh[...]) + dot_t(hi, sl[...]), close.reshape(NY, 8, 256)
 
     lax.fori_loop(1, NM, source_wait, 0)
-    ring_send(0, jnp.sum(sr[...].astype(F32).reshape(NY, NCH, 8, 256), axis=1))
+    arrived = jnp.sum(sr[...].astype(F32).reshape(NY, NCH, 8, 256), axis=1)
+    mz[0, my_z, 0:32] = arrived[:, :, 0:128].reshape(32, 128)
+    ring_start(0, pl.ds(0, 32))
+    ring_tail(0, arrived[:, :, 128:256])
     ring_wait(0)
     ident = cm[:, 128 + ID_LANE: 128 + ID_LANE + 1].astype(jnp.int32)
     match = jnp.where((ident == col >> 2) & ((row & 3) == (col & 3)), 1.0, 0.0).astype(BF16)
     pick[...] = dot_t(eye[...], match).astype(BF16)
-    r[...] = collect()
+    near[...] = dot_t(own[...].astype(BF16), match).astype(BF16)
+    start_r, start_f = collect()
+    r[...] = start_r
+    ff[...] = start_f
 
     def across(a):
         a = a + pltpu.roll(a, 64, 1)
         return a + pltpu.roll(a, 32, 1)
 
-    def spread_near(grid):
-        hi, lo = halves(grid)
-        choose = own[...].astype(BF16)
-        near_hi = dot(choose, hi).astype(BF16)
-        near_lo = dot(choose, lo).astype(BF16)
-        field = dot(near_hi, sh[...]) + dot(near_lo, sh[...]) + dot(near_hi, sl[...])
-        ts[...] = field.reshape(NY, 8, 256)
-
     def widen(y):
         for h in range(LH):
-            base = ts[y, :, 0:128] if h < 32 else ts[y, :, 128:256]
+            base = ff[y, :, 0:128] if h < 32 else ff[y, :, 128:256]
             fx[y, :, lanes(h)] = jnp.take_along_axis(base, 4 * (h % 32) + (lane >> 5), axis=1)
 
-    def predict_one(m, y):
-        parts = [None] * 4
+    def group_terms(slot, y, factors):
+        acc = []
         for h in range(LH):
-            prod = jr[m, :, lanes(h)].astype(F32) * fx[y, :, lanes(h)]
-            parts[h % 4] = prod if parts[h % 4] is None else parts[h % 4] + prod
-        return across((parts[0] + parts[1]) + (parts[2] + parts[3]))
-
-    def terms(slot):
-        def group(y, carry):
-            acc = []
-            for h in range(LH):
-                total = None
-                for c in range(NCH):
-                    prod = jr[y * NCH + c, :, lanes(h)].astype(F32) * sv[y * NCH + c]
-                    total = prod if total is None else total + prod
-                acc.append(total)
-            hi, lo = halves(jnp.concatenate(acc, axis=0))
-            sums = dot(hi, spot[...]) + dot(lo, spot[...])
-            first = jnp.zeros((8, 128), F32)
-            second = jnp.zeros((8, 128), F32)
-            for h in range(LH):
-                piece = jnp.where(lane >> 2 == h % 32, sums[8 * h: 8 * h + 8], 0.0)
-                if h < 32:
-                    first = first + piece
-                else:
-                    second = second + piece
-            ts[y, :, 0:128] = first
-            ts[y, :, 128:256] = second
-            return carry
-
-        lax.fori_loop(0, NY, group, 0)
-        hi, lo = halves(ts[...].reshape(32, 256))
-        back = dot_t(hi, sh[...]) + dot_t(lo, sh[...]) + dot_t(hi, sl[...])
-        ring_send(slot, back.reshape(NY, 8, 256))
-
-    spread_near(r[...])
+            total = None
+            for c in range(NCH):
+                prod = jf[y * NCH + c, :, lanes(h)] * factors[c]
+                total = prod if total is None else total + prod
+            acc.append(total)
+        hi, lo = halves(jnp.concatenate(acc, axis=0))
+        sums = dot(hi, spot[...]) + dot(lo, spot[...])
+        first = jnp.zeros((8, 128), F32)
+        second = jnp.zeros((8, 128), F32)
+        for h in range(LH):
+            piece = jnp.where(lane >> 2 == h % 32, sums[8 * h: 8 * h + 8], 0.0)
+            if h < 32:
+                first = first + piece
+            else:
+                second = second + piece
+        part = pl.ds(pl.multiple_of(8 * y, 8), 8)
+        mz[slot, my_z, part] = first
+        g[part, 0:128] = second
+        ring_start(slot, part)
+
+    def send_tail(slot):
+        ring_tail(slot, [g[8 * y: 8 * y + 8, 0:128] for y in range(NY)])
 
     def widen_group(y, carry):
         widen(y)
@@ -306,10 +301,19 @@
     lax.fori_loop(0, NY, widen_group, 0)
 
     def first_predict(m):
+        y = m // NCH
         extra = jr[m, :, lanes(LH - 1)].astype(F32)
         weights = across(jnp.where((lane >= 32) & (lane < 96), extra, 0.0))
         mw[m] = weights
-        sv[m] = weights * predict_one(m, m // NCH)
+        parts = [None] * 4
+        for h in range(LH):
+            tile = jr[m, :, lanes(h)].astype(F32)
+            if h == LH - 1:
+                tile = jnp.where(lane < 32, tile, 0.0)
+            jf[m, :, lanes(h)] = tile
+            prod = tile * fx[y, :, lanes(h)]
+            parts[h % 4] = prod if parts[h % 4] is None else parts[h % 4] + prod
+        sv[m] = weights * across((parts[0] + parts[1]) + (parts[2] + parts[3]))
 
     first_predict(my_m)
 
@@ -322,13 +326,22 @@
         return carry
 
     lax.fori_loop(1, NM, arrive, 0)
-    terms(1)
+
+    def first_group(y, carry):
+        group_terms(1, y, [sv[y * NCH + c] for c in range(NCH)])
+        return carry
+
+    lax.fori_loop(0, NY, first_group, 0)
+    send_tail(1)
     p[...] = jnp.zeros_like(p)
     s[...] = jnp.zeros_like(s)
     x[...] = jnp.zeros_like(x)
     v[...] = jnp.zeros_like(v)
+    fv[...] = jnp.zeros_like(fv)
     ring_wait(1)
-    w[...] = r[...] + collect()
+    more, close = collect()
+    ff[...] = ff[...] + close
+    w[...] = r[...] + more
 
     def plane_copy(slot, t, arriving):
         m = (my_m + t) % NM
@@ -353,7 +366,7 @@
 
         lax.fori_loop(1, NM, start, 0)
 
-    def advance(i, slot, norm_old, step_old):
+    def scalars_wait(i, slot, norm_old, step_old):
         def finish(t, carry):
             plane_copy(slot, t, True).wait()
             return carry
@@ -364,44 +377,54 @@
         bend = jnp.sum(jnp.where(lane1 < 64, 0.0, both), axis=1, keepdims=True)
         ratio = jnp.where(i == 0, 0.0, norm / norm_old)
         step = norm / (bend - jnp.where(i == 0, 0.0, ratio * norm / step_old))
+        return norm, step, ratio
+
+    def iteration(i, carry):
+        slot = i & 1
+        scalars_send(slot)
+
+        def group(y, carry):
+            widen(y)
+            totals = [None] * NCH
+            for h in range(LH):
+                wide = fx[y, :, lanes(h)]
+                for c in range(NCH):
+                    prod = jf[y * NCH + c, :, lanes(h)] * wide
+                    totals[c] = prod if totals[c] is None else totals[c] + prod
+            group_terms(slot, y, [mw[y * NCH + c] * across(totals[c]) for c in range(NCH)])
+            return carry
+
+        lax.fori_loop(0, NY, group, 0)
+        send_tail(slot)
+        norm, step, ratio = scalars_wait(i, slot, *carry)
         turned = w[...] + ratio * s[...]
         s[...] = turned
         ahead = r[...] + ratio * p[...]
         p[...] = ahead
         x[...] = x[...] + step * ahead
         r[...] = r[...] - step * turned
-        return norm, step, ratio
-
-    def iteration(i, carry):
-        slot = i & 1
-        spread_near(w[...])
-        scalars_send(slot)
-
-        def predict(y, carry):
-            widen(y)
-            for c in range(NCH):
-                m = y * NCH + c
-                sv[m] = mw[m] * predict_one(m, y)
-            return carry
-
-        lax.fori_loop(0, NY, predict, 0)
-        terms(slot)
-        norm, step, ratio = advance(i, slot, *carry)
         ring_wait(slot)
-        along = w[...] + collect() + ratio * v[...]
+        more, close = collect()
+        along = ff[...] + close + ratio * fv[...]
+        fv[...] = along
+        ff[...] = ff[...] - step * along
+        along = w[...] + more + ratio * v[...]
         v[...] = along
         w[...] = w[...] - step * along
         return norm, step
 
     one = jnp.ones((1, 1), F32)
     norm, step = lax.fori_loop(0, ITERS - 1, iteration, (one, one))
-    scalars_send((ITERS - 1) & 1)
-    advance(ITERS - 1, (ITERS - 1) & 1, norm, step)
-
-    hi, lo = halves(x[...])
-    grown = dot(hi, sh[...]) + dot(lo, sh[...]) + dot(hi, sl[...])
+    last = ITERS - 1
+    scalars_send(last & 1)
+    cm[...] = times(r[...], sh, sl)
+    v[...] = times(p[...], sh, sl)
+    g[...] = times(x[...], sh, sl)
+    norm, step, ratio = scalars_wait(last, last & 1, norm, step)
+    grown = g[...] + step * (cm[...] + ratio * v[...])
+    left = r[...] - step * (w[...] + ratio * s[...])
     out[:, 0:8, :] = grown.astype(BF16).reshape(NM, 8, 256)
-    out[:, 8:16, :] = r[...].astype(BF16).reshape(NM, 8, 256)
+    out[:, 8:16, :] = left.astype(BF16).reshape(NM, 8, 256)
 
     def result_copy(t, arriving):
         m = (my_m + t) % NM
@@ -448,20 +471,23 @@
             pltpu.VMEM((L, L), F32),
             pltpu.VMEM((NM, 8, WIDE), BF16),
             pltpu.VMEM((NM, 8, WIDE), BF16),
+            pltpu.VMEM((NM, 8, WIDE), F32),
             pltpu.VMEM((NM, 8, 128), F32),
             pltpu.VMEM((NY, 8, WIDE), F32),
             pltpu.VMEM((NM, 8, 128), F32),
             pltpu.VMEM((NY, 8, 256), F32),
-            table, table, table, table,
+            pltpu.VMEM((NY, 8, 256), F32),
+            table, table, table, table, table, table,
             pltpu.VMEM((128, 128), BF16),
             pltpu.VMEM((32, 256), F32),
+            pltpu.VMEM((32, 256), BF16),
             table,
             pltpu.VMEM((NY, 8, 128), F32),
             pltpu.VMEM((144, 256), F32),
             pltpu.VMEM((NM, 8, 256), BF16),
             pltpu.VMEM((NM, 8, 256), BF16),
             state,
-            state, state, state, state, state, state,
+            state, state, state, state, state, state, state,
             pltpu.VMEM((2, NZ, 40, 128), F32),
             pltpu.VMEM((2, NM, 1, 128), F32),
             pltpu.VMEM((NM, 16, 256), BF16),

time: 112 us -> 112 us (level)
  no operation moved by 1% of the time
where the time goes in v3:
time: 112 us
  Pallas kernels  107 us (96%)
  local copies, waits for them, and re-layouts  3.16 us (3%)
  between operations  1.29 us (1%)
    pallas_call x1, Pallas kernels, per_device(): pl.pallas_call(kernel, out_shape=(jax.ShapeDtypeStruct((L, 256), F32),) *...  107 us
    unnamed x2, local copies, waits for them, and re-layouts  3.16 us

profile of v3, /device:TPU:1, one launch (start us, length us, event | category | flops | bytes accessed | tf_op | source)
XLA Modules:
  0.0 111.6 jit_solution(10926265886841314210)
XLA Ops:
  1.3 107.2 %cg.1 = (f32[137,256]{1,0:T(8,128)}, f32[137,256]{1,0:T(8,128)}) custom-call(s32[1]{0:T(128)S(6)} %copy.10.cnt_hbm, s32[2]{0:T(128)} %gb_hbm.1, bf16[137,32,256]{2,1,0:T(8,128)(2,1)} %bitcast.3, f32[32,256]{1,0:T(8,128)} %w_hbm.1, f32[32,256]{1,0:T(8,128)} %d_hbm.1, f32[137,137]{1,0:T(8,128)} %s_hbm.1), custom_call_target="tpu_custom_call" | custom-call | tf_op jit(solution)/shard_map/cg/pallas_call | solution.py:460
  108.4 1.6 %copy.11 = f32[256,137]{0,1:T(8,128)} copy(f32[256,137]{0,1:T(8,128)} %bitcast.5) | data formatting | bytes 280576
  110.0 1.6 %copy.12 = f32[256,137]{0,1:T(8,128)} copy(f32[256,137]{0,1:T(8,128)} %bitcast.4) | data formatting | bytes 280576

commit v4 on v3

--- a/solution.py
+++ b/solution.py
@@ -1,3 +1,5 @@
+import functools
+
 import jax
 import jax.numpy as jnp
 from jax import lax
@@ -46,7 +48,7 @@
 
 def kernel(
     cnt_hbm, gb_hbm, jt_hbm, w_hbm, d_hbm, s_hbm,
-    inc_ref, res_ref,
+    got_ref,
     cnt_ref, gb_ref, jv, w_ref, d_ref, s_ref,
     sb, jr, jf, mw, fx, sv, ff, fv, sh, sl, qh, ql, perm, eye, spot, own, near, pick, ids, tt, so, sr, cm,
     r, p, s, x, w, v, g, mz, sx, out, got,
@@ -63,11 +65,10 @@
         for k, (a, b) in enumerate((
             (w_hbm, w_ref), (d_hbm, d_ref), (cnt_hbm, cnt_ref), (gb_hbm, gb_ref), (s_hbm, s_ref)))
     ]
-    blocks = []
-    for q in range(CHUNKS):
-        first, last = 4 * PER * q, min(4 * PER * (q + 1), L)
-        blocks.append(pltpu.make_async_copy(
-            jt_hbm.at[first:last], jv.at[first:last], fs.at[len(fetches) + q]))
+    blocks = [
+        pltpu.make_async_copy(jt_hbm.at[first:last], jv.at[first:last], fs.at[len(fetches) + q])
+        for q, (first, last) in enumerate(((0, 4 * PER), (4 * PER, L)))
+    ]
     for copy in (blocks[0], *fetches, *blocks[1:]):
         copy.start()
 
@@ -104,23 +105,30 @@
         sb[:, :, pl.ds(pl.multiple_of(h * 128, 128), 128)] = turned.reshape(NM, 8, 128)
         return carry
 
-    def send_part(first, last):
-        part = pl.ds(first * 128, (last - first) * 128)
-
+    def chunk(q):
+        return pl.ds(q * PER * 128, PER * 128)
+
+    def send_chunk(q):
         def send(t, carry):
             m = (my_m + t) % NM
             pltpu.make_async_remote_copy(
-                src_ref=sb.at[m, :, part], dst_ref=jr.at[my_m, :, part],
-                send_sem=js.at[m], recv_sem=jq.at[my_m],
+                src_ref=sb.at[m, :, chunk(q)], dst_ref=jr.at[my_m, :, chunk(q)],
+                send_sem=js.at[m], recv_sem=jq.at[q, my_m],
                 device_id=plane_peer(m), device_id_type=MESH).start()
             return carry
 
         lax.fori_loop(1, NM, send, 0)
+
+    def chunk_wait(q, m):
+        pltpu.make_async_remote_copy(
+            src_ref=sb.at[m, :, chunk(q)], dst_ref=jr.at[m, :, chunk(q)],
+            send_sem=js.at[m], recv_sem=jq.at[q, m],
+            device_id=plane_peer(m), device_id_type=MESH).wait_recv()
 
     blocks[0].wait()
     lax.fori_loop(0, PER, turn, 0, unroll=True)
     pl.semaphore_wait(barrier, NM - 1 + NZ - 1)
-    send_part(0, PER)
+    send_chunk(0)
 
     for copy in fetches:
         copy.wait()
@@ -175,10 +183,14 @@
     lax.fori_loop(1, NM, source_send, 0)
     sr[my_m] = so[my_m]
 
-    lax.fori_loop(PER, LH - 1, turn, 0, unroll=9)
-    block = jnp.concatenate([jv[L - 1], weight_hi, weight_lo, jnp.zeros_like(weight_hi)], axis=0)
-    sb[:, :, lanes(LH - 1)] = dot_t(perm[...], block).astype(BF16).reshape(NM, 8, 128)
-    send_part(PER, LH)
+    for q in range(1, CHUNKS):
+        if q < CHUNKS - 1:
+            lax.fori_loop(q * PER, (q + 1) * PER, turn, 0, unroll=True)
+        else:
+            lax.fori_loop(q * PER, LH - 1, turn, 0, unroll=True)
+            block = jnp.concatenate([jv[L - 1], weight_hi, weight_lo, jnp.zeros_like(weight_hi)], axis=0)
+            sb[:, :, lanes(LH - 1)] = dot_t(perm[...], block).astype(BF16).reshape(NM, 8, 128)
+        send_chunk(q)
     jr[my_m] = sb[my_m]
 
     eye[...] = jnp.where(row == col, 1.0, 0.0).astype(BF16)
@@ -245,11 +257,51 @@
         hi, lo = halves(dot(pick[...], hi) + dot(pick[...], lo))
         return dot_t(hi, sh[...]) + dot_t(lo, sh[...]) + dot_t(hi, sl[...]), close.reshape(NY, 8, 256)
 
+    def across(a):
+        a = a + pltpu.roll(a, 64, 1)
+        return a + pltpu.roll(a, 32, 1)
+
+    def convert(q, m):
+        tile = jr[m, :, chunk(q)].astype(F32)
+        if q == CHUNKS - 1:
+            extra = tile[:, (PER - 1) * 128:]
+            mw[m] = across(jnp.where((lane >= 32) & (lane < 96), extra, 0.0))
+            tile = jnp.concatenate([tile[:, : (PER - 1) * 128], jnp.where(lane < 32, extra, 0.0)], axis=1)
+        jf[m, :, chunk(q)] = tile
+        return tile
+
+    def predict_part(q, m, tile):
+        wide = tile * fx[m // NCH, :, chunk(q)]
+        total = wide[:, 0:128]
+        for h in range(1, PER):
+            total = total + wide[:, 128 * h: 128 * h + 128]
+        sv[m] = total if q == 0 else sv[m] + total
+
+    def every_piece(q, work, waits):
+        def pair(t, carry):
+            m = (my_m + NM - 2 * t) % NM
+            n = (my_m + NM - 2 * t - 1) % NM
+            if waits:
+                chunk_wait(q, m)
+                chunk_wait(q, n)
+            work(m)
+            work(n)
+            return carry
+
+        first = (my_m + NM - 1) % NM
+        if waits:
+            chunk_wait(q, first)
+        work(my_m)
+        work(first)
+        lax.fori_loop(1, NM // 2, pair, 0)
+
+    every_piece(0, functools.partial(convert, 0), True)
     lax.fori_loop(1, NM, source_wait, 0)
     arrived = jnp.sum(sr[...].astype(F32).reshape(NY, NCH, 8, 256), axis=1)
     mz[0, my_z, 0:32] = arrived[:, :, 0:128].reshape(32, 128)
     ring_start(0, pl.ds(0, 32))
     ring_tail(0, arrived[:, :, 128:256])
+    every_piece(1, functools.partial(convert, 1), True)
     ring_wait(0)
     ident = cm[:, 128 + ID_LANE: 128 + ID_LANE + 1].astype(jnp.int32)
     match = jnp.where((ident == col >> 2) & ((row & 3) == (col & 3)), 1.0, 0.0).astype(BF16)
@@ -258,10 +310,6 @@
     start_r, start_f = collect()
     r[...] = start_r
     ff[...] = start_f
-
-    def across(a):
-        a = a + pltpu.roll(a, 64, 1)
-        return a + pltpu.roll(a, 32, 1)
 
     def widen(y):
         for h in range(LH):
@@ -300,39 +348,25 @@
 
     lax.fori_loop(0, NY, widen_group, 0)
 
-    def first_predict(m):
-        y = m // NCH
-        extra = jr[m, :, lanes(LH - 1)].astype(F32)
-        weights = across(jnp.where((lane >= 32) & (lane < 96), extra, 0.0))
-        mw[m] = weights
-        parts = [None] * 4
-        for h in range(LH):
-            tile = jr[m, :, lanes(h)].astype(F32)
-            if h == LH - 1:
-                tile = jnp.where(lane < 32, tile, 0.0)
-            jf[m, :, lanes(h)] = tile
-            prod = tile * fx[y, :, lanes(h)]
-            parts[h % 4] = prod if parts[h % 4] is None else parts[h % 4] + prod
-        sv[m] = weights * across((parts[0] + parts[1]) + (parts[2] + parts[3]))
-
-    first_predict(my_m)
-
-    def arrive(t, carry):
-        m = (my_m + NM - t) % NM
+    for q in (0, 1):
+        every_piece(q, lambda m: predict_part(q, m, jf[m, :, chunk(q)]), False)
+    for q in range(2, CHUNKS):
+        every_piece(q, lambda m: predict_part(q, m, convert(q, m)), True)
+
+    def sent(t, carry):
+        m = (my_m + t) % NM
         pltpu.make_async_remote_copy(
-            src_ref=sb.at[m], dst_ref=jr.at[m], send_sem=js.at[m], recv_sem=jq.at[m],
-            device_id=plane_peer(m), device_id_type=MESH).wait()
-        first_predict(m)
-        return carry
-
-    lax.fori_loop(1, NM, arrive, 0)
+            src_ref=sb.at[m], dst_ref=jr.at[m], send_sem=js.at[m], recv_sem=jq.at[0, m],
+            device_id=plane_peer(m), device_id_type=MESH).wait_send()
+        return carry
 
     def first_group(y, carry):
-        group_terms(1, y, [sv[y * NCH + c] for c in range(NCH)])
+        group_terms(1, y, [mw[y * NCH + c] * across(sv[y * NCH + c]) for c in range(NCH)])
         return carry
 
     lax.fori_loop(0, NY, first_group, 0)
     send_tail(1)
+    lax.fori_loop(1, NM, sent, 0)
     p[...] = jnp.zeros_like(p)
     s[...] = jnp.zeros_like(s)
     x[...] = jnp.zeros_like(x)
@@ -445,10 +479,18 @@
     lax.fori_loop(1, NM, give, 0)
     got[my_m] = out[my_y * NZ + my_z]
     lax.fori_loop(1, NM, take, 0)
+    got_ref[...] = got[...]
+
+
+def finish(got_ref, inc_ref, res_ref):
+    row = iota((256, 256), 0)
+    col = iota((256, 256), 1)
+    order = jnp.where(
+        ((row & 4) << 5) + ((row >> 3) << 2) + (row & 3) == col, 1.0, 0.0).astype(BF16)
+    eye = jnp.where(iota((144, 256), 0) == iota((144, 256), 1), 1.0, 0.0).astype(BF16)
     for k, ref in ((0, inc_ref), (1, res_ref)):
-        rows = got[:, 8 * k: 8 * k + 8, :].reshape(256, 256)
-        flat = dot_t(eye[0:144, :], rows).astype(BF16)
-        ref[...] = dot(flat, perm[...])[0:L]
+        rows = got_ref[:, 8 * k: 8 * k + 8, :].reshape(256, 256)
+        ref[...] = dot(dot_t(eye, rows).astype(BF16), order)[0:L]
 
 
 def per_device(jacobian, departures, obs_weights, column_count, grid_block, sqrt_cov):
@@ -457,11 +499,11 @@
     dma = pltpu.SemaphoreType.DMA
     state = pltpu.VMEM((256, 256), F32)
     table = pltpu.VMEM((256, 256), BF16)
-    inc, res = pl.pallas_call(
+    got = pl.pallas_call(
         kernel,
-        out_shape=(jax.ShapeDtypeStruct((L, 256), F32),) * 2,
+        out_shape=jax.ShapeDtypeStruct((NM, 16, 256), BF16),
         in_specs=[pl.BlockSpec(memory_space=pltpu.HBM)] * 6,
-        out_specs=(vmem, vmem),
+        out_specs=vmem,
         scratch_shapes=[
             pltpu.SMEM((1,), jnp.int32),
             pltpu.SMEM((2,), jnp.int32),
@@ -492,8 +534,8 @@
             pltpu.VMEM((2, NM, 1, 128), F32),
             pltpu.VMEM((NM, 16, 256), BF16),
             pltpu.VMEM((NM, 16, 256), BF16),
-            dma((5 + CHUNKS,)),
-            dma((NM,)), dma((NM,)),
+            dma((7,)),
+            dma((NM,)), dma((CHUNKS, NM)),
             dma((NM,)), dma((NM,)),
             dma((2, NZ)), dma((2, NZ)),
             dma((2, NM)), dma((2, NM)),
@@ -504,6 +546,13 @@
             collective_id=0, has_side_effects=True, vmem_limit_bytes=67_000_000),
         name="cg",
     )(column_count, grid_block, jt, obs_weights, departures, sqrt_cov)
+    inc, res = pl.pallas_call(
+        finish,
+        out_shape=(jax.ShapeDtypeStruct((L, 256), F32),) * 2,
+        in_specs=[vmem],
+        out_specs=(vmem, vmem),
+        name="order",
+    )(got)
     return inc.T, res.T
 
 

time: 112 us -> 105 us (0.938)
  local copies, waits for them, and re-layouts: 3.16 us -> 0 us
  Pallas kernels: 107 us -> 104 us
    unnamed x2 -> x0, local copies, waits for them, and re-layouts: 3.16 us -> none
    pallas_call x1 -> x2, Pallas kernels: 107 us -> 104 us  [the longest x1 102 us: per_device(): pl.pallas_call(kernel, out_shape=jax.ShapeDtypeStruct((NM, 16, 256), BF16...]
where the time goes in v4:
time: 105 us
  Pallas kernels  104 us (99%)
  between operations  1.29 us (1%)
    pallas_call x1, Pallas kernels, per_device(): pl.pallas_call(kernel, out_shape=jax.ShapeDtypeStruct((NM, 16, 256), BF16...  102 us
    pallas_call x1, Pallas kernels, per_device(): pl.pallas_call(finish, out_shape=(jax.ShapeDtypeStruct((L, 256), F32),) *...  2.14 us

profile of v4, /device:TPU:1, one launch (start us, length us, event | category | flops | bytes accessed | tf_op | source)
XLA Modules:
  0.0 105.3 jit_solution(13220390753205572966)
XLA Ops:
  1.3 101.9 %cg.1.got_ref = bf16[32,16,256]{2,1,0:T(8,128)(2,1)} custom-call(s32[1]{0:T(128)S(6)} %copy.8.cnt_hbm, s32[2]{0:T(128)} %gb_hbm.1, bf16[137,32,256]{2,1,0:T(8,128)(2,1)} %bitcast.3, f32[32,256]{1,0:T(8,128)} %w_hbm.1, f32[32,256]{1,0:T(8,128)} %d_hbm.1, f32[137,137]{1,0:T(8,128)} %s_hbm.1), custom_call_target="tpu_custom_call" | custom-call | tf_op jit(solution)/shard_map/cg/pallas_call | solution.py:502
  103.1 2.1 %order.1 = (f32[137,256]{1,0:T(8,128)}, f32[137,256]{1,0:T(8,128)}) custom-call(bf16[32,16,256]{2,1,0:T(8,128)(2,1)} %cg.1.got_ref), custom_call_target="tpu_custom_call" | custom-call | tf_op jit(solution)/shard_map/order/pallas_call | solution.py:549

commit v5 on v4

--- a/solution.py
+++ b/solution.py
@@ -50,7 +50,7 @@
     cnt_hbm, gb_hbm, jt_hbm, w_hbm, d_hbm, s_hbm,
     got_ref,
     cnt_ref, gb_ref, jv, w_ref, d_ref, s_ref,
-    sb, jr, jf, mw, fx, sv, ff, fv, sh, sl, qh, ql, perm, eye, spot, own, near, pick, ids, tt, so, sr, cm,
+    sb, jr, jf, mw, fx, sv, pn, pv, sc, ff, sh, sl, qh, ql, perm, eye, spot, own, near, pick, ids, tt, so, sr, cm,
     r, p, s, x, w, v, g, mz, sx, out, got,
     fs, js, jq, as_, aq, zs, zq, xs, xq, ys, yq, os, oq,
 ):
@@ -73,7 +73,13 @@
         copy.start()
 
     def plane_peer(m):
-        return (m // NCH, my_z, (m % NCH) // NC, m % NC)
+        return (m >> 3, my_z, (m >> 1) & 3, m & 1)
+
+    def ahead_by(t):
+        return (((my_y + (t >> 2)) & 3) << 3) + (((my_x + t) & 3) << 1) + ((my_c + (t >> 4)) & 1)
+
+    def behind_by(t):
+        return (((my_y - (t >> 2)) & 3) << 3) + (((my_x - t) & 3) << 1) + ((my_c + (t >> 4)) & 1)
 
     def ring_peer(z):
         return (my_y, z, my_x, my_c)
@@ -81,11 +87,11 @@
     barrier = pltpu.get_barrier_semaphore()
 
     def greet_plane(t, carry):
-        pl.semaphore_signal(barrier, inc=1, device_id=plane_peer((my_m + t) % NM), device_id_type=MESH)
+        pl.semaphore_signal(barrier, inc=1, device_id=plane_peer((my_m + t) & 31), device_id_type=MESH)
         return carry
 
     def greet_ring(t, carry):
-        pl.semaphore_signal(barrier, inc=1, device_id=ring_peer((my_z + t) % NZ), device_id_type=MESH)
+        pl.semaphore_signal(barrier, inc=1, device_id=ring_peer((my_z + t) & 7), device_id_type=MESH)
         return carry
 
     lax.fori_loop(1, NM, greet_plane, 0)
@@ -110,7 +116,7 @@
 
     def send_chunk(q):
         def send(t, carry):
-            m = (my_m + t) % NM
+            m = ahead_by(t)
             pltpu.make_async_remote_copy(
                 src_ref=sb.at[m, :, chunk(q)], dst_ref=jr.at[my_m, :, chunk(q)],
                 send_sem=js.at[m], recv_sem=jq.at[q, my_m],
@@ -141,7 +147,7 @@
     ids[my_y] = jnp.where(r4 < 4, gb_ref[0], gb_ref[1]).astype(F32)
 
     def id_copy(t, arriving):
-        peer = (my_y + t) % NY
+        peer = (my_y + t) & 3
         at = peer if arriving else my_y
         return pltpu.make_async_remote_copy(
             src_ref=ids.at[at], dst_ref=ids.at[at], send_sem=ys.at[t], recv_sem=yq.at[at],
@@ -169,18 +175,14 @@
     flat = dot_t(perm[...], hi) + dot_t(perm[...], lo)
     so[...] = jnp.pad(flat, ((0, 0), (0, 112))).astype(BF16).reshape(NM, 8, 256)
 
-    def source_copy(t, arriving):
-        m = (my_m + t) % NM
-        return pltpu.make_async_remote_copy(
-            src_ref=so.at[m], dst_ref=sr.at[m if arriving else my_m],
-            send_sem=as_.at[m], recv_sem=aq.at[m if arriving else my_m],
-            device_id=plane_peer(m), device_id_type=MESH)
-
     def source_send(t, carry):
-        source_copy(t, False).start()
-        return carry
-
-    lax.fori_loop(1, NM, source_send, 0)
+        m = (my_m + t) & 31
+        pltpu.make_async_remote_copy(
+            src_ref=so.at[m], dst_ref=sr.at[my_m], send_sem=as_.at[0], recv_sem=aq.at[0],
+            device_id=plane_peer(m), device_id_type=MESH).start()
+        return carry
+
+    lax.fori_loop(1, NM, source_send, 0, unroll=True)
     sr[my_m] = so[my_m]
 
     for q in range(1, CHUNKS):
@@ -209,12 +211,14 @@
         own[pl.ds(8 * y, 8), :] = jnp.where(
             (ident == lane2 >> 2) & ((row2 & 3) == (lane2 & 3)), 1.0, 0.0)
 
-    def source_wait(t, carry):
-        source_copy(t, True).wait()
-        return carry
+    def source_wait():
+        pltpu.make_async_remote_copy(
+            src_ref=so.at[pl.ds(0, NM - 1)], dst_ref=sr.at[pl.ds(0, NM - 1)],
+            send_sem=as_.at[0], recv_sem=aq.at[0],
+            device_id=plane_peer(my_m ^ 1), device_id_type=MESH).wait()
 
     def ring_copy(slot, t, arriving):
-        z = (my_z + t) % NZ
+        z = (my_z + t) & 7
         at = z if arriving else my_z
         return pltpu.make_async_remote_copy(
             src_ref=mz.at[slot, at], dst_ref=mz.at[slot, at],
@@ -226,7 +230,7 @@
             pltpu.make_async_remote_copy(
                 src_ref=mz.at[slot, my_z, part], dst_ref=mz.at[slot, my_z, part],
                 send_sem=zs.at[slot, t], recv_sem=zq.at[slot, my_z],
-                device_id=ring_peer((my_z + t) % NZ), device_id_type=MESH).start()
+                device_id=ring_peer((my_z + t) & 7), device_id_type=MESH).start()
 
     def ring_tail(slot, tails):
         packed = None
@@ -251,11 +255,14 @@
         hi, lo = halves(a)
         return dot(hi, hi_ref[...]) + dot(lo, hi_ref[...]) + dot(hi, lo_ref[...])
 
-    def collect():
+    def near_field():
         hi, lo = halves(cm[...])
-        close = times(dot(near[...], hi) + dot(near[...], lo), qh, ql)
+        return times(dot(near[...], hi) + dot(near[...], lo), qh, ql).reshape(NY, 8, 256)
+
+    def collected():
+        hi, lo = halves(cm[...])
         hi, lo = halves(dot(pick[...], hi) + dot(pick[...], lo))
-        return dot_t(hi, sh[...]) + dot_t(lo, sh[...]) + dot_t(hi, sl[...]), close.reshape(NY, 8, 256)
+        return dot_t(hi, sh[...]) + dot_t(lo, sh[...]) + dot_t(hi, sl[...])
 
     def across(a):
         a = a + pltpu.roll(a, 64, 1)
@@ -271,7 +278,7 @@
         return tile
 
     def predict_part(q, m, tile):
-        wide = tile * fx[m // NCH, :, chunk(q)]
+        wide = tile * fx[m >> 3, :, chunk(q)]
         total = wide[:, 0:128]
         for h in range(1, PER):
             total = total + wide[:, 128 * h: 128 * h + 128]
@@ -279,8 +286,8 @@
 
     def every_piece(q, work, waits):
         def pair(t, carry):
-            m = (my_m + NM - 2 * t) % NM
-            n = (my_m + NM - 2 * t - 1) % NM
+            m = behind_by(2 * t)
+            n = behind_by(2 * t + 1)
             if waits:
                 chunk_wait(q, m)
                 chunk_wait(q, n)
@@ -288,7 +295,7 @@
             work(n)
             return carry
 
-        first = (my_m + NM - 1) % NM
+        first = behind_by(1)
         if waits:
             chunk_wait(q, first)
         work(my_m)
@@ -296,7 +303,7 @@
         lax.fori_loop(1, NM // 2, pair, 0)
 
     every_piece(0, functools.partial(convert, 0), True)
-    lax.fori_loop(1, NM, source_wait, 0)
+    source_wait()
     arrived = jnp.sum(sr[...].astype(F32).reshape(NY, NCH, 8, 256), axis=1)
     mz[0, my_z, 0:32] = arrived[:, :, 0:128].reshape(32, 128)
     ring_start(0, pl.ds(0, 32))
@@ -307,9 +314,8 @@
     match = jnp.where((ident == col >> 2) & ((row & 3) == (col & 3)), 1.0, 0.0).astype(BF16)
     pick[...] = dot_t(eye[...], match).astype(BF16)
     near[...] = dot_t(own[...].astype(BF16), match).astype(BF16)
-    start_r, start_f = collect()
-    r[...] = start_r
-    ff[...] = start_f
+    ff[...] = near_field()
+    r[...] = collected()
 
     def widen(y):
         for h in range(LH):
@@ -354,14 +360,16 @@
         every_piece(q, lambda m: predict_part(q, m, convert(q, m)), True)
 
     def sent(t, carry):
-        m = (my_m + t) % NM
+        m = (my_m + t) & 31
         pltpu.make_async_remote_copy(
             src_ref=sb.at[m], dst_ref=jr.at[m], send_sem=js.at[m], recv_sem=jq.at[0, m],
             device_id=plane_peer(m), device_id_type=MESH).wait_send()
         return carry
 
     def first_group(y, carry):
-        group_terms(1, y, [mw[y * NCH + c] * across(sv[y * NCH + c]) for c in range(NCH)])
+        for c in range(NCH):
+            sv[y * NCH + c] = across(sv[y * NCH + c])
+        group_terms(1, y, [mw[y * NCH + c] * sv[y * NCH + c] for c in range(NCH)])
         return carry
 
     lax.fori_loop(0, NY, first_group, 0)
@@ -371,19 +379,20 @@
     s[...] = jnp.zeros_like(s)
     x[...] = jnp.zeros_like(x)
     v[...] = jnp.zeros_like(v)
-    fv[...] = jnp.zeros_like(fv)
-    ring_wait(1)
-    more, close = collect()
-    ff[...] = ff[...] + close
-    w[...] = r[...] + more
-
-    def plane_copy(slot, t, arriving):
-        m = (my_m + t) % NM
-        at = m if arriving else my_m
-        return pltpu.make_async_remote_copy(
-            src_ref=sx.at[slot, at], dst_ref=sx.at[slot, at],
-            send_sem=xs.at[slot, m], recv_sem=xq.at[slot, at],
-            device_id=plane_peer(m), device_id_type=MESH)
+    pv[...] = jnp.zeros_like(pv)
+    sc[...] = jnp.where(iota((8, 128), 0) == 0, -1.0, 0.0)
+
+    def plane_start(slot, t):
+        pltpu.make_async_remote_copy(
+            src_ref=sx.at[slot, my_m], dst_ref=sx.at[slot, my_m],
+            send_sem=xs.at[slot], recv_sem=xq.at[slot],
+            device_id=plane_peer((my_m + t) & 31), device_id_type=MESH).start()
+
+    def plane_wait(slot):
+        most = sx.at[slot, pl.ds(0, NM - 1)]
+        pltpu.make_async_remote_copy(
+            src_ref=most, dst_ref=most, send_sem=xs.at[slot], recv_sem=xq.at[slot],
+            device_id=plane_peer(my_m ^ 1), device_id_type=MESH).wait()
 
     def scalars_send(slot):
         res = r[...]
@@ -394,30 +403,49 @@
         sx[slot, my_m] = jnp.where(
             lane1 < 64, norm + pltpu.roll(norm, 64, 1), bend + pltpu.roll(bend, 64, 1))
 
-        def start(t, carry):
-            plane_copy(slot, t, False).start()
-            return carry
-
-        lax.fori_loop(1, NM, start, 0)
-
-    def scalars_wait(i, slot, norm_old, step_old):
-        def finish(t, carry):
-            plane_copy(slot, t, True).wait()
-            return carry
-
-        lax.fori_loop(1, NM, finish, 0)
+        for t in range(1, NM):
+            plane_start(slot, t)
+
+    def scalars_keep(i):
+        slot = i & 1
+        step_old, norm_old = sc[0:1, 0:1], sc[2:3, 0:1]
+
+        plane_wait(slot)
         both = jnp.sum(sx[slot], axis=0)
         norm = jnp.sum(jnp.where(lane1 < 64, both, 0.0), axis=1, keepdims=True)
         bend = jnp.sum(jnp.where(lane1 < 64, 0.0, both), axis=1, keepdims=True)
         ratio = jnp.where(i == 0, 0.0, norm / norm_old)
         step = norm / (bend - jnp.where(i == 0, 0.0, ratio * norm / step_old))
-        return norm, step, ratio
+        place = iota((8, 128), 0)
+        sc[...] = jnp.where(place == 0, step, jnp.where(place == 1, ratio, norm))
+
+    def catch_up(i, step, ratio):
+        more = collected()
+
+        @pl.when(i == 0)
+        def start_w():
+            w[...] = r[...] + more
+
+        @pl.when(i > 0)
+        def move():
+            old = w[...]
+            turned = old + ratio * s[...]
+            s[...] = turned
+            ahead = r[...] + ratio * p[...]
+            p[...] = ahead
+            x[...] = x[...] + step * ahead
+            r[...] = r[...] - step * turned
+            along = old + more + ratio * v[...]
+            v[...] = along
+            w[...] = old - step * along
+
+        scalars_send(i & 1)
 
     def iteration(i, carry):
-        slot = i & 1
-        scalars_send(slot)
-
-        def group(y, carry):
+        ring_wait((i + 1) & 1)
+        ff[...] = near_field()
+
+        def predict(y, carry):
             widen(y)
             totals = [None] * NCH
             for h in range(LH):
@@ -425,60 +453,66 @@
                 for c in range(NCH):
                     prod = jf[y * NCH + c, :, lanes(h)] * wide
                     totals[c] = prod if totals[c] is None else totals[c] + prod
-            group_terms(slot, y, [mw[y * NCH + c] * across(totals[c]) for c in range(NCH)])
+            for c in range(NCH):
+                pn[y * NCH + c] = across(totals[c])
             return carry
 
+        lax.fori_loop(0, NY, predict, 0)
+
+        @pl.when(i > 0)
+        def scalars():
+            scalars_keep(i - 1)
+
+        step, ratio = sc[0:1, 0:1], sc[1:2, 0:1]
+        begun = jnp.where(i > 0, 1.0, 0.0)
+
+        def group(y, carry):
+            factors = []
+            for c in range(NCH):
+                m = y * NCH + c
+                old = sv[m]
+                along = begun * old + pn[m] + ratio * pv[m]
+                pv[m] = along
+                new = old - step * along
+                sv[m] = new
+                factors.append(mw[m] * new)
+            group_terms(i & 1, y, factors)
+            return carry
+
         lax.fori_loop(0, NY, group, 0)
-        send_tail(slot)
-        norm, step, ratio = scalars_wait(i, slot, *carry)
-        turned = w[...] + ratio * s[...]
-        s[...] = turned
-        ahead = r[...] + ratio * p[...]
-        p[...] = ahead
-        x[...] = x[...] + step * ahead
-        r[...] = r[...] - step * turned
-        ring_wait(slot)
-        more, close = collect()
-        along = ff[...] + close + ratio * fv[...]
-        fv[...] = along
-        ff[...] = ff[...] - step * along
-        along = w[...] + more + ratio * v[...]
-        v[...] = along
-        w[...] = w[...] - step * along
-        return norm, step
-
-    one = jnp.ones((1, 1), F32)
-    norm, step = lax.fori_loop(0, ITERS - 1, iteration, (one, one))
+        send_tail(i & 1)
+        catch_up(i, step, ratio)
+        return carry
+
+    lax.fori_loop(0, ITERS - 1, iteration, 0)
     last = ITERS - 1
-    scalars_send(last & 1)
+    ring_wait(last + 1 & 1)
+    scalars_keep(last - 1)
+    catch_up(last, sc[0:1, 0:1], sc[1:2, 0:1])
     cm[...] = times(r[...], sh, sl)
     v[...] = times(p[...], sh, sl)
     g[...] = times(x[...], sh, sl)
-    norm, step, ratio = scalars_wait(last, last & 1, norm, step)
+    scalars_keep(last)
+    step, ratio = sc[0:1, 0:1], sc[1:2, 0:1]
     grown = g[...] + step * (cm[...] + ratio * v[...])
     left = r[...] - step * (w[...] + ratio * s[...])
     out[:, 0:8, :] = grown.astype(BF16).reshape(NM, 8, 256)
     out[:, 8:16, :] = left.astype(BF16).reshape(NM, 8, 256)
 
-    def result_copy(t, arriving):
-        m = (my_m + t) % NM
-        at = m if arriving else my_m
-        return pltpu.make_async_remote_copy(
-            src_ref=out.at[m // NCH * NZ + my_z], dst_ref=got.at[at],
-            send_sem=os.at[m], recv_sem=oq.at[at],
-            device_id=plane_peer(m), device_id_type=MESH)
-
     def give(t, carry):
-        result_copy(t, False).start()
-        return carry
-
-    def take(t, carry):
-        result_copy(t, True).wait()
-        return carry
-
-    lax.fori_loop(1, NM, give, 0)
+        m = (my_m + t) & 31
+        pltpu.make_async_remote_copy(
+            src_ref=out.at[((m >> 3) << 3) + my_z], dst_ref=got.at[my_m],
+            send_sem=os.at[0], recv_sem=oq.at[0],
+            device_id=plane_peer(m), device_id_type=MESH).start()
+        return carry
+
+    lax.fori_loop(1, NM, give, 0, unroll=True)
     got[my_m] = out[my_y * NZ + my_z]
-    lax.fori_loop(1, NM, take, 0)
+    pltpu.make_async_remote_copy(
+        src_ref=out.at[pl.ds(0, NM - 1)], dst_ref=got.at[pl.ds(0, NM - 1)],
+        send_sem=os.at[0], recv_sem=oq.at[0],
+        device_id=plane_peer(my_m ^ 1), device_id_type=MESH).wait()
     got_ref[...] = got[...]
 
 
@@ -517,7 +551,9 @@
             pltpu.VMEM((NM, 8, 128), F32),
             pltpu.VMEM((NY, 8, WIDE), F32),
             pltpu.VMEM((NM, 8, 128), F32),
-            pltpu.VMEM((NY, 8, 256), F32),
+            pltpu.VMEM((NM, 8, 128), F32),
+            pltpu.VMEM((NM, 8, 128), F32),
+            pltpu.VMEM((8, 128), F32),
             pltpu.VMEM((NY, 8, 256), F32),
             table, table, table, table, table, table,
             pltpu.VMEM((128, 128), BF16),
@@ -536,11 +572,11 @@
             pltpu.VMEM((NM, 16, 256), BF16),
             dma((7,)),
             dma((NM,)), dma((CHUNKS, NM)),
-            dma((NM,)), dma((NM,)),
+            dma((1,)), dma((1,)),
             dma((2, NZ)), dma((2, NZ)),
-            dma((2, NM)), dma((2, NM)),
+            dma((2,)), dma((2,)),
             dma((NY,)), dma((NY,)),
-            dma((NM,)), dma((NM,)),
+            dma((1,)), dma((1,)),
         ],
         compiler_params=pltpu.CompilerParams(
             collective_id=0, has_side_effects=True, vmem_limit_bytes=67_000_000),

time: 105 us -> 99.1 us (0.944)
  Pallas kernels: 104 us -> 97.7 us
    pallas_call x1, Pallas kernels: 102 us -> 95.5 us  [per_device(): pl.pallas_call(kernel, out_shape=jax.ShapeDtypeStruct((NM, 16, 256), BF16...]
where the time goes in v5:
time: 99.1 us; the launch traced here: 98.9 us
  Pallas kernels  97.7 us (99%)
  between operations  1.29 us (1%)
    pallas_call x1, Pallas kernels, per_device(): pl.pallas_call(kernel, out_shape=jax.ShapeDtypeStruct((NM, 16, 256), BF16...  95.5 us
    pallas_call x1, Pallas kernels, per_device(): pl.pallas_call(finish, out_shape=(jax.ShapeDtypeStruct((L, 256), F32),) *...  2.14 us

profile of v5, /device:TPU:1, one launch (start us, length us, event | category | flops | bytes accessed | tf_op | source)
XLA Modules:
  0.0 98.9 jit_solution(11766438205608434416)
XLA Ops:
  1.3 95.5 %cg.1.got_ref = bf16[32,16,256]{2,1,0:T(8,128)(2,1)} custom-call(s32[1]{0:T(128)S(6)} %copy.8.cnt_hbm, s32[2]{0:T(128)} %gb_hbm.1, bf16[137,32,256]{2,1,0:T(8,128)(2,1)} %bitcast.3, f32[32,256]{1,0:T(8,128)} %w_hbm.1, f32[32,256]{1,0:T(8,128)} %d_hbm.1, f32[137,137]{1,0:T(8,128)} %s_hbm.1), custom_call_target="tpu_custom_call" | custom-call | tf_op jit(solution)/shard_map/cg/pallas_call | solution.py:536
  96.8 2.1 %order.1 = (f32[137,256]{1,0:T(8,128)}, f32[137,256]{1,0:T(8,128)}) custom-call(bf16[32,16,256]{2,1,0:T(8,128)(2,1)} %cg.1.got_ref), custom_call_target="tpu_custom_call" | custom-call | tf_op jit(solution)/shard_map/order/pallas_call | solution.py:585

commit v6 on v5

--- a/solution.py
+++ b/solution.py
@@ -14,7 +14,7 @@
 NCH = NX * NC
 NM = NY * NCH
 LH = 35
-CHUNKS = 5
+CHUNKS = 7
 PER = LH // CHUNKS
 WIDE = LH * 128
 ID_LANE = 16
@@ -94,8 +94,8 @@
         pl.semaphore_signal(barrier, inc=1, device_id=ring_peer((my_z + t) & 7), device_id_type=MESH)
         return carry
 
-    lax.fori_loop(1, NM, greet_plane, 0)
-    lax.fori_loop(1, NZ, greet_ring, 0)
+    lax.fori_loop(1, NM, greet_plane, 0, unroll=True)
+    lax.fori_loop(1, NZ, greet_ring, 0, unroll=True)
 
     row = iota((256, 256), 0)
     col = iota((256, 256), 1)
@@ -119,22 +119,25 @@
             m = ahead_by(t)
             pltpu.make_async_remote_copy(
                 src_ref=sb.at[m, :, chunk(q)], dst_ref=jr.at[my_m, :, chunk(q)],
-                send_sem=js.at[m], recv_sem=jq.at[q, my_m],
+                send_sem=js.at[0], recv_sem=jq.at[q, my_m],
                 device_id=plane_peer(m), device_id_type=MESH).start()
             return carry
 
-        lax.fori_loop(1, NM, send, 0)
+        lax.fori_loop(1, NM, send, 0, unroll=True)
 
     def chunk_wait(q, m):
         pltpu.make_async_remote_copy(
             src_ref=sb.at[m, :, chunk(q)], dst_ref=jr.at[m, :, chunk(q)],
-            send_sem=js.at[m], recv_sem=jq.at[q, m],
+            send_sem=js.at[0], recv_sem=jq.at[q, m],
             device_id=plane_peer(m), device_id_type=MESH).wait_recv()
 
     blocks[0].wait()
     lax.fori_loop(0, PER, turn, 0, unroll=True)
     pl.semaphore_wait(barrier, NM - 1 + NZ - 1)
     send_chunk(0)
+    blocks[1].wait()
+    lax.fori_loop(PER, 2 * PER, turn, 0, unroll=True)
+    send_chunk(1)
 
     for copy in fetches:
         copy.wait()
@@ -162,8 +165,6 @@
     scaled_d = (weight * d_ref[...]).astype(BF16)
     d_ref[...] = scaled_d.astype(F32)
 
-    for copy in blocks[1:]:
-        copy.wait()
 
     def gather_source(g, carry):
         part = jv[pl.ds(8 * g, 8)].astype(F32) * d_ref[...][None]
@@ -185,7 +186,7 @@
     lax.fori_loop(1, NM, source_send, 0, unroll=True)
     sr[my_m] = so[my_m]
 
-    for q in range(1, CHUNKS):
+    for q in range(2, CHUNKS):
         if q < CHUNKS - 1:
             lax.fori_loop(q * PER, (q + 1) * PER, turn, 0, unroll=True)
         else:
@@ -217,19 +218,11 @@
             send_sem=as_.at[0], recv_sem=aq.at[0],
             device_id=plane_peer(my_m ^ 1), device_id_type=MESH).wait()
 
-    def ring_copy(slot, t, arriving):
-        z = (my_z + t) & 7
-        at = z if arriving else my_z
-        return pltpu.make_async_remote_copy(
-            src_ref=mz.at[slot, at], dst_ref=mz.at[slot, at],
-            send_sem=zs.at[slot, t], recv_sem=zq.at[slot, at],
-            device_id=ring_peer(z), device_id_type=MESH)
-
     def ring_start(slot, part):
         for t in (4, 3, 5, 2, 6, 1, 7):
             pltpu.make_async_remote_copy(
                 src_ref=mz.at[slot, my_z, part], dst_ref=mz.at[slot, my_z, part],
-                send_sem=zs.at[slot, t], recv_sem=zq.at[slot, my_z],
+                send_sem=zs.at[slot], recv_sem=zq.at[slot],
                 device_id=ring_peer((my_z + t) & 7), device_id_type=MESH).start()
 
     def ring_tail(slot, tails):
@@ -242,8 +235,10 @@
         ring_start(slot, pl.ds(32, 8))
 
     def ring_wait(slot):
-        for t in range(1, NZ):
-            ring_copy(slot, t, True).wait()
+        most = mz.at[slot, pl.ds(0, NZ - 1)]
+        pltpu.make_async_remote_copy(
+            src_ref=most, dst_ref=most, send_sem=zs.at[slot], recv_sem=zq.at[slot],
+            device_id=ring_peer((my_z + 1) & 7), device_id_type=MESH).wait()
         for z in range(NZ):
             cm[32 * z: 32 * z + 32, 0:128] = mz[slot, z, 0:32]
             packed = mz[slot, z, 32:40]
@@ -359,13 +354,6 @@
     for q in range(2, CHUNKS):
         every_piece(q, lambda m: predict_part(q, m, convert(q, m)), True)
 
-    def sent(t, carry):
-        m = (my_m + t) & 31
-        pltpu.make_async_remote_copy(
-            src_ref=sb.at[m], dst_ref=jr.at[m], send_sem=js.at[m], recv_sem=jq.at[0, m],
-            device_id=plane_peer(m), device_id_type=MESH).wait_send()
-        return carry
-
     def first_group(y, carry):
         for c in range(NCH):
             sv[y * NCH + c] = across(sv[y * NCH + c])
@@ -374,7 +362,9 @@
 
     lax.fori_loop(0, NY, first_group, 0)
     send_tail(1)
-    lax.fori_loop(1, NM, sent, 0)
+    pltpu.make_async_remote_copy(
+        src_ref=sb.at[pl.ds(0, NM - 1)], dst_ref=jr.at[pl.ds(0, NM - 1)], send_sem=js.at[0],
+        recv_sem=jq.at[0, 0], device_id=plane_peer(my_m ^ 1), device_id_type=MESH).wait_send()
     p[...] = jnp.zeros_like(p)
     s[...] = jnp.zeros_like(s)
     x[...] = jnp.zeros_like(x)
@@ -571,9 +561,9 @@
             pltpu.VMEM((NM, 16, 256), BF16),
             pltpu.VMEM((NM, 16, 256), BF16),
             dma((7,)),
-            dma((NM,)), dma((CHUNKS, NM)),
+            dma((1,)), dma((CHUNKS, NM)),
             dma((1,)), dma((1,)),
-            dma((2, NZ)), dma((2, NZ)),
+            dma((2,)), dma((2,)),
             dma((2,)), dma((2,)),
             dma((NY,)), dma((NY,)),
             dma((1,)), dma((1,)),

time: 99.1 us -> 98.2 us (level)
  no operation moved by 1% of the time
where the time goes in v6:
time: 98.2 us; the launch traced here: 98.1 us
  Pallas kernels  96.8 us (99%)
  between operations  1.29 us (1%)
    pallas_call x1, Pallas kernels, per_device(): pl.pallas_call(kernel, out_shape=jax.ShapeDtypeStruct((NM, 16, 256), BF16...  94.7 us
    pallas_call x1, Pallas kernels, per_device(): pl.pallas_call(finish, out_shape=(jax.ShapeDtypeStruct((L, 256), F32),) *...  2.14 us

profile of v6, /device:TPU:1, one launch (start us, length us, event | category | flops | bytes accessed | tf_op | source)
XLA Modules:
  0.0 98.1 jit_solution(15960601434698867449)
XLA Ops:
  1.3 94.7 %cg.1.got_ref = bf16[32,16,256]{2,1,0:T(8,128)(2,1)} custom-call(s32[1]{0:T(128)S(6)} %copy.8.cnt_hbm, s32[2]{0:T(128)} %gb_hbm.1, bf16[137,32,256]{2,1,0:T(8,128)(2,1)} %bitcast.3, f32[32,256]{1,0:T(8,128)} %w_hbm.1, f32[32,256]{1,0:T(8,128)} %d_hbm.1, f32[137,137]{1,0:T(8,128)} %s_hbm.1), custom_call_target="tpu_custom_call" | custom-call | tf_op jit(solution)/shard_map/cg/pallas_call | solution.py:526
  96.0 2.1 %order.1 = (f32[137,256]{1,0:T(8,128)}, f32[137,256]{1,0:T(8,128)}) custom-call(bf16[32,16,256]{2,1,0:T(8,128)(2,1)} %cg.1.got_ref), custom_call_target="tpu_custom_call" | custom-call | tf_op jit(solution)/shard_map/order/pallas_call | solution.py:575

commit v7 on v6

--- a/solution.py
+++ b/solution.py
@@ -436,10 +436,11 @@
         ff[...] = near_field()
 
         def predict(y, carry):
-            widen(y)
             totals = [None] * NCH
+            field = ff[y]
             for h in range(LH):
-                wide = fx[y, :, lanes(h)]
+                base = field[:, 0:128] if h < 32 else field[:, 128:256]
+                wide = jnp.take_along_axis(base, 4 * (h % 32) + (lane >> 5), axis=1)
                 for c in range(NCH):
                     prod = jf[y * NCH + c, :, lanes(h)] * wide
                     totals[c] = prod if totals[c] is None else totals[c] + prod
@@ -447,7 +448,7 @@
                 pn[y * NCH + c] = across(totals[c])
             return carry
 
-        lax.fori_loop(0, NY, predict, 0)
+        lax.fori_loop(0, NY, predict, 0, unroll=2)
 
         @pl.when(i > 0)
         def scalars():
@@ -469,7 +470,7 @@
             group_terms(i & 1, y, factors)
             return carry
 
-        lax.fori_loop(0, NY, group, 0)
+        lax.fori_loop(0, NY, group, 0, unroll=2)
         send_tail(i & 1)
         catch_up(i, step, ratio)
         return carry

time: 98.2 us -> 96.7 us (0.985)
  Pallas kernels: 96.8 us -> 95.3 us
    pallas_call x1, Pallas kernels: 94.7 us -> 93.2 us  [per_device(): pl.pallas_call(kernel, out_shape=jax.ShapeDtypeStruct((NM, 16, 256), BF16...]
where the time goes in v7:
time: 96.7 us; the launch traced here: 96.6 us
  Pallas kernels  95.3 us (99%)
  between operations  1.29 us (1%)
    pallas_call x1, Pallas kernels, per_device(): pl.pallas_call(kernel, out_shape=jax.ShapeDtypeStruct((NM, 16, 256), BF16...  93.2 us
    pallas_call x1, Pallas kernels, per_device(): pl.pallas_call(finish, out_shape=(jax.ShapeDtypeStruct((L, 256), F32),) *...  2.14 us

profile of v7, /device:TPU:1, one launch (start us, length us, event | category | flops | bytes accessed | tf_op | source)
XLA Modules:
  0.0 96.6 jit_solution(14158819113458384030)
XLA Ops:
  1.3 93.2 %cg.1.got_ref = bf16[32,16,256]{2,1,0:T(8,128)(2,1)} custom-call(s32[1]{0:T(128)S(6)} %copy.8.cnt_hbm, s32[2]{0:T(128)} %gb_hbm.1, bf16[137,32,256]{2,1,0:T(8,128)(2,1)} %bitcast.3, f32[32,256]{1,0:T(8,128)} %w_hbm.1, f32[32,256]{1,0:T(8,128)} %d_hbm.1, f32[137,137]{1,0:T(8,128)} %s_hbm.1), custom_call_target="tpu_custom_call" | custom-call | tf_op jit(solution)/shard_map/cg/pallas_call | solution.py:527
  94.5 2.1 %order.1 = (f32[137,256]{1,0:T(8,128)}, f32[137,256]{1,0:T(8,128)}) custom-call(bf16[32,16,256]{2,1,0:T(8,128)(2,1)} %cg.1.got_ref), custom_call_target="tpu_custom_call" | custom-call | tf_op jit(solution)/shard_map/order/pallas_call | solution.py:576
